TPU v7x, 32 devices: a whole 2x2x4 slice. The times are simulated.
32 devices in a mesh: gz: 8 (over y, x, core), gy: 4 (over z).
Axes of the slice: x: 2, y: 2, z: 4, core: 2. Of those that a mesh axis runs over, the one named last changes fastest.
Arguments:
- coarse_density: float32 [96, 96, 96], P(None, 'gy'), may hold values from -4 to 4
- density_in: float32 [192, 36864], P('gz', 'gy'), may hold values from -9 to 9
- history: float32 [8, 192, 36864], P(None, 'gz', 'gy'), may hold values from -12 to 12
- atom_cell: int32 [8, 4, 1], P('gz', 'gy'), may hold values from 0 to 221183
- atom_offset: float32 [3, 8, 4, 1], P(None, 'gz', 'gy'), may hold values from 0 to 1
- atom_charge: float32 [8, 4, 1], P('gz', 'gy'), may hold values from -16 to 16
- atom_width: float32 [8, 4, 1], P('gz', 'gy'), may hold values from 0.25 to 1
Outputs:
- residual: float32 [192, 36864], P('gz', 'gy')
- potential: float32 [192, 36864], P('gz', 'gy')
- intersections: float32 [9], replicated
Inputs may be any that keep to these rules, and one draw needn't show every extreme that they name: `atom_cell`: the cell lies inside the block of 24 x 48 x 192 fine cells of the slot's first two indices.
All inputs are finite; a program needn't handle non-finite values.
Results may differ from a plain program's by a relative error of at most 0.0003.
Values sent between devices are 32-bit elements; how exact they have to be, the bound alone decides.
No kernel may reach another device: no remote copies, remote signals or barrier semaphores. Data moves between devices by JAX's collectives and lax.ppermute only.
A program may use at most 64 MiB of HBM per device.

v0:
```python
import math

import jax
import jax.numpy as jnp
import numpy as np
from jax import lax
from jax.experimental import pallas as pl
from jax.experimental.pallas import tpu as pltpu
from jax.sharding import PartitionSpec as P

RC = 4
NF = 192


def with_halo(block, sides, width):
    for axis, dim in sides:
        count = lax.axis_size(axis)
        forward = [(i, i + 1) for i in range(count - 1)]
        forward.append((count - 1, 0))
        backward = [(target, source) for source, target in forward]
        low = lax.ppermute(
            lax.slice_in_dim(block, block.shape[dim] - width, None, axis=dim), axis, forward
        )
        high = lax.ppermute(lax.slice_in_dim(block, 0, width, axis=dim), axis, backward)
        block = jnp.concatenate([low, block, high], axis=dim)
    return block


def midpoint(extended, dimension, cells_in):

    def window(offset):
        return lax.slice_in_dim(extended, offset, offset + cells_in, axis=dimension)

    even_cells = window(2)
    odd_cells = (9.0 * (window(2) + window(3)) - window(1) - window(4)) / 16.0
    merged = jnp.stack([even_cells, odd_cells], dimension + 1)
    new_shape = list(even_cells.shape)
    new_shape[dimension] = 2 * cells_in
    return merged.reshape(new_shape)


def signed(counter, length):
    return jnp.where(counter < length // 2, counter, counter - length)


def shape_value(squared, charge, exponent):
    factor = charge * (exponent / jnp.pi) ** 1.5
    return factor * jnp.maximum(
        jnp.exp(-exponent * squared) - jnp.exp(-exponent * float(RC * RC)), 0.0
    )


def gaussians(dist_z, dist_y, dist_x, charge, exponent):
    squared = (
        dist_z[:, :, None, None] ** 2
        + dist_y[:, None, :, None] ** 2
        + dist_x[:, None, None, :] ** 2
    )
    return jnp.sum(
        shape_value(squared, charge[:, None, None, None], exponent[:, None, None, None]), 0
    )


def tables(length):
    counter = jnp.arange(length, dtype=jnp.int32)
    phase = counter[:, None] * counter[None, :] % length
    angle = 2.0 * jnp.pi / length * phase.astype(jnp.float32)
    return (jnp.cos(angle), jnp.sin(angle))


def contract(values, table, dimension):
    product = jnp.tensordot(values, table, axes=([dimension], [0]), precision=lax.Precision.HIGHEST)
    return jnp.moveaxis(product, -1, dimension)


def transform(spectra, dimension, direction):
    cosine, sine_table = tables(spectra.shape[dimension])
    inner_dim = dimension - 1
    real_part = spectra[:, 0]
    imag_part = spectra[:, 1]
    new_real = contract(real_part, cosine, inner_dim) - direction * contract(
        imag_part, sine_table, inner_dim
    )
    new_imag = contract(imag_part, cosine, inner_dim) + direction * contract(
        real_part, sine_table, inner_dim
    )
    result = jnp.stack([new_real, new_imag], 1)
    if direction > 0:
        result = result / spectra.shape[dimension]
    return result


def transform_y(pieces):
    return transform(pieces, 3, -1.0)


def transform_z(pieces):
    return transform(pieces, 2, -1.0)


def inverse_y(pieces):
    return transform(pieces, 3, 1.0)


def inverse_x_real(pieces):
    cosine, sine_table = tables(pieces.shape[4])
    real_part = contract(pieces[:, 0], cosine, 3) - contract(pieces[:, 1], sine_table, 3)
    return real_part / pieces.shape[4]


def forward(fields):
    cosine, sine_table = tables(fields.shape[3])
    spectra = jnp.stack([contract(fields, cosine, 3), -contract(fields, sine_table, 3)], 1)
    columns = transform_y(lax.all_to_all(spectra, "gy", split_axis=4, concat_axis=3, tiled=True))
    return transform_z(lax.all_to_all(columns, "gz", split_axis=3, concat_axis=2, tiled=True))


def inverse(spectra):
    local_z = transform(spectra, 2, 1.0)
    rows_back = inverse_y(lax.all_to_all(local_z, "gz", split_axis=2, concat_axis=3, tiled=True))
    return inverse_x_real(lax.all_to_all(rows_back, "gy", split_axis=3, concat_axis=4, tiled=True))


def poisson_weight(spectra):
    length = spectra.shape[2]
    y_block = spectra.shape[3]
    x_block = spectra.shape[4]
    wave_z = signed(jnp.arange(length, dtype=jnp.int32), length)
    wave_y = signed(lax.axis_index("gz") * y_block + jnp.arange(y_block, dtype=jnp.int32), length)
    wave_x = signed(lax.axis_index("gy") * x_block + jnp.arange(x_block, dtype=jnp.int32), length)
    squares = (
        wave_z[:, None, None] * wave_z[:, None, None]
        + wave_y[None, :, None] * wave_y[None, :, None]
        + wave_x[None, None, :] * wave_x[None, None, :]
    )
    scaled = (2.0 * jnp.pi / length) ** 2 * jnp.maximum(squares, 1).astype(jnp.float32)
    return jnp.where(squares > 0, 4.0 * jnp.pi / scaled, 0.0)


def total_intersections(own_terms):
    return lax.psum(own_terms, ("gz", "gy"))


def deposit_rims(atom_cell, atom_offset, atom_charge, atom_width, slab_z, slab_y, length):
    cell_ids = atom_cell.reshape(-1)
    local_z = cell_ids // (slab_y * length)
    local_y = cell_ids // length % slab_y
    local_x = cell_ids % length
    offsets = atom_offset.reshape(3, -1)
    dist_z = (jnp.arange(slab_z + 2 * RC, dtype=jnp.int32)[None, :] - RC - local_z[:, None]).astype(
        jnp.float32
    ) - offsets[0][:, None]
    dist_y = (jnp.arange(slab_y + 2 * RC, dtype=jnp.int32)[None, :] - RC - local_y[:, None]).astype(
        jnp.float32
    ) - offsets[1][:, None]
    dist_x = (
        signed(
            (jnp.arange(length, dtype=jnp.int32)[None, :] - local_x[:, None]) % length, length
        ).astype(jnp.float32)
        - offsets[2][:, None]
    )
    buffer_sum = gaussians(dist_z, dist_y, dist_x, atom_charge.reshape(-1), atom_width.reshape(-1))
    rims_z = jnp.concatenate([buffer_sum[:RC], buffer_sum[-RC:]], 0)
    near_z = with_halo(rims_z, (("gz", 0),), RC)
    middle = buffer_sum[RC : RC + slab_z]
    middle = middle.at[:RC].add(near_z[:RC]).at[slab_z - RC :].add(near_z[3 * RC :])
    rims_y = jnp.concatenate([middle[:, :RC], middle[:, -RC:]], 1)
    near_y = with_halo(rims_y, (("gy", 1),), RC)
    inside = middle[:, RC : RC + slab_y]
    return inside.at[:, :RC].add(near_y[:, :RC]).at[:, slab_y - RC :].add(near_y[:, 3 * RC :])


def local(coarse_density, density_in, history, atom_cell, atom_offset, atom_charge, atom_width):
    length = NF
    slab_z = density_in.shape[0]
    slab_y = density_in.shape[1] // length
    density_cube = density_in.reshape(slab_z, slab_y, length)
    history_cube = history.reshape(history.shape[0], slab_z, slab_y, length)
    extended = with_halo(coarse_density, (("gy", 1),), 2)
    coarse_rows = coarse_density.shape[0] // lax.axis_size("gz")
    beside_all = jnp.concatenate([extended[-2:], extended, extended[:2]], 0)
    start = lax.axis_index("gz") * coarse_rows
    own_planes = lax.dynamic_slice_in_dim(beside_all, start, coarse_rows + 4, 0)
    wrapped = jnp.concatenate([own_planes[:, :, -2:], own_planes, own_planes[:, :, :2]], 2)
    smooth = midpoint(wrapped, 2, coarse_density.shape[2])
    smooth = midpoint(smooth, 1, coarse_density.shape[1])
    smooth = midpoint(smooth, 0, coarse_rows)
    charge_field = deposit_rims(
        atom_cell, atom_offset, atom_charge, atom_width, slab_z, slab_y, length
    )
    residual = smooth + charge_field - density_cube
    cells_all = float(length) ** 3
    spectra = forward(residual[None])
    weight = poisson_weight(spectra)
    potential = inverse(weight * spectra)[0]
    own_terms = (
        jnp.concatenate(
            [
                jnp.sum(history_cube * potential[None], axis=(1, 2, 3)),
                jnp.sum(residual * potential)[None],
            ]
        )
        / cells_all
    )
    intersections = total_intersections(own_terms)
    return (
        residual.reshape(slab_z, slab_y * length),
        potential.reshape(slab_z, slab_y * length),
        intersections,
    )


GROUP = 16
LANES = 128
SUB = 8


def basis(length):
    half = length // 2
    wave = np.concatenate([np.arange(half + 1), np.arange(1, half)])
    angle = 2.0 * np.pi / length * (np.outer(wave, np.arange(length)) % length)
    rows = np.where(np.arange(length)[:, None] <= half, np.cos(angle), np.sin(angle))
    scale = np.where((wave == 0) | (wave == half), 1.0, np.sqrt(2.0)) / np.sqrt(length)
    return rows * scale[:, None], wave


def split_table(table):
    table = np.asarray(table, np.float32)
    high = table.astype(jnp.bfloat16)
    low = (table - high.astype(np.float32)).astype(jnp.bfloat16)
    return jnp.asarray(np.stack([high, low]))


def halves(values):
    high = values.astype(jnp.bfloat16)
    return high, (values - high.astype(jnp.float32)).astype(jnp.bfloat16)


def thirds(values):
    high = values.astype(jnp.bfloat16)
    rest = values - high.astype(jnp.float32)
    middle = rest.astype(jnp.bfloat16)
    return high, middle, (rest - middle.astype(jnp.float32)).astype(jnp.bfloat16)


NN = (((1,), (0,)), ((), ()))
NT = (((1,), (1,)), ((), ()))


def mm(left, right, dims):
    return lax.dot_general(left, right, dims, preferred_element_type=jnp.float32)


def mm3(left, right, dims=NN):
    return (
        mm(left[0], right[1], dims) + mm(left[1], right[0], dims) + mm(left[0], right[0], dims)
    )


def tile_masks():
    row = lax.broadcasted_iota(jnp.int32, (SUB, LANES), 0)
    group = lax.broadcasted_iota(jnp.int32, (SUB, LANES), 1) // SUB
    return row, group


def rotate_up(upper, lower, masks):
    row, group = masks
    bit = (group & 8) != 0
    upper, lower = jnp.where(bit, lower, upper), jnp.where(bit, upper, lower)
    for shift in (4, 2, 1):
        bit = (group & shift) != 0
        roll_u = pltpu.roll(upper, SUB - shift, 0)
        roll_l = pltpu.roll(lower, SUB - shift, 0)
        stay = row < SUB - shift
        new_u = jnp.where(stay, roll_u, roll_l)
        new_l = jnp.where(stay, roll_l, roll_u)
        upper, lower = jnp.where(bit, new_u, upper), jnp.where(bit, new_l, lower)
    return upper, lower


def skew(values, start):
    return pltpu.roll(values, start, 1, stride=SUB, stride_axis=0)


def block_turn(upper, lower, masks):
    upper, lower = rotate_up(skew(upper, 0), skew(lower, 64), masks)
    return skew(upper, 0), skew(lower, 64)


class Plan:
    def __init__(self, mesh_shape, length, coarse, fz, fy):
        self.nz, self.ny = mesh_shape
        self.count = self.nz * self.ny
        self.length, self.coarse, self.fz, self.fy = length, coarse, fz, fy
        self.j = length // self.count
        self.zo, self.yo = fz // SUB, fy // GROUP
        self.main = self.j * self.zo * self.yo
        self.tail = self.main + self.j
        self.rows_out = self.tail + 4
        self.rows_back = -(-self.main // SUB) * SUB
        self.ext = length + 24

    def ok(self):
        return (
            (self.nz, self.ny, self.zo, self.yo, self.j) == (8, 4, 3, 3, 6)
            and self.fz % SUB == 0
            and self.fy % GROUP == 0
            and self.length == self.coarse * 2
            and self.rows_out % SUB == 0
        )


def ext_slot(edge, zo):
    return ((15, 3, 1)[edge] + 5 * zo) % GROUP


def fast_tables(plan):
    length, nz = plan.length, plan.nz
    rows, wave = basis(length)
    fine_of = np.zeros((plan.coarse, length), np.float32)
    for i in range(plan.coarse):
        fine_of[i, 2 * i] += 1.0
        for step, value in ((0, 9), (1, 9), (-1, -1), (2, -1)):
            fine_of[(i + step) % plan.coarse, 2 * i + 1] += value / 16.0
    local_z = np.zeros((plan.fz, GROUP), np.float32)
    for i in range(plan.fz // 2):
        local_z[2 * i, i + 1] = 1.0
        for step, value in ((1, 9), (2, 9), (0, -1), (3, -1)):
            local_z[2 * i + 1, i + step] += value / 16.0

    def along_z(turn):
        half_of, owner = turn // SUB, turn % SUB
        lane = np.arange(SUB)
        z_main = (owner[:, None] * plan.fz + half_of[:, None] * SUB + lane[None]).reshape(-1)
        z_shared = (owner[:, None] * plan.fz + 2 * SUB + lane[None]).reshape(-1)
        odd = np.repeat(half_of, SUB)
        tables_z = []
        for parity in (0, 1):
            table = np.zeros((2 * LANES, length))
            table[:LANES] = rows[:, z_main].T
            table[LANES:] = np.where((odd == parity)[:, None], rows[:, z_shared].T, 0.0)
            tables_z.append(table)
        return tables_z, (z_main, z_shared, odd)

    z_tables, z_lanes = along_z(np.arange(GROUP))
    z_back = along_z((-np.arange(GROUP)) % GROUP)[0]
    y_of_row = (np.arange(plan.ext) - SUB) % length
    lanes = np.zeros((SUB, LANES), np.float32)
    lanes[0], lanes[1], lanes[2] = z_lanes
    squares = (wave.astype(np.float64) ** 2).astype(np.float32)
    x_window = np.zeros((plan.count, length + GROUP, SUB), np.float32)
    x_of_row = (np.arange(length + GROUP) - SUB) % length
    for d in range(plan.count):
        for j in range(plan.j):
            x_window[d, :, j] = rows[j * plan.count + d, x_of_row]
    return {
        "x": split_table(rows),
        "fine": jnp.asarray(fine_of, jnp.bfloat16),
        "kron": jnp.asarray(np.kron(np.eye(SUB), local_z), jnp.bfloat16),
        "z": split_table(np.stack(z_tables)),
        "zt": split_table(np.stack([t.T for t in z_back])),
        "y": split_table(rows[:, y_of_row]),
        "yt": split_table(rows.T),
        "lanes": jnp.asarray(lanes),
        "wave": jnp.asarray(np.stack([np.broadcast_to(squares, (SUB, length))])),
        "wave_c": jnp.asarray(np.broadcast_to(squares[:, None], (length, LANES))),
        "window": jnp.asarray(x_window.reshape(plan.count, -1)),
    }


def part_a(plan):
    length, fz, fy, count = plan.length, plan.fz, plan.fy, plan.count
    rows_c = fy // 2
    per = plan.rows_out

    def kernel(cell, offset, charge, width, coarse, density, fine, kron, xt, send, partial, planes, smooth, field):
        a = lax.axis_index("gz")
        b = lax.axis_index("gy")
        own = plan.coarse // plan.nz
        for t in range(GROUP):
            planes[pl.ds(t * rows_c, rows_c), :] = coarse[lax.rem(own * a + plan.coarse - 1 + t, plan.coarse)]
        for part in range(rows_c // SUB):
            block = jnp.concatenate(
                [planes[pl.ds(part * SUB + y, GROUP, stride=rows_c), :] for y in range(SUB)], 0
            )
            wide = sum(mm(piece, fine[...], NN) for piece in thirds(block)[::-1])
            tall = sum(mm(kron[...], piece, NN) for piece in thirds(wide)[::-1])
            for y in range(SUB):
                smooth[part * SUB + y] = tall[y * fz : (y + 1) * fz]

        def row(i):
            return smooth[i] if 0 <= i < rows_c else jnp.zeros((fz, length), jnp.float32)

        for i in range(rows_c):
            odd_row = (9.0 * (row(i) + row(i + 1)) - row(i - 1) - row(i + 2)) * (1.0 / 16.0)
            old = density[:, 2 * i * length : (2 * i + 2) * length]
            even_out = smooth[i] - old[:, :length]
            odd_out = odd_row - old[:, length:]
            field[2 * i] = even_out
            field[2 * i + 1] = odd_out
            partial[:, 2 * i * length : (2 * i + 2) * length] = jnp.concatenate([even_out, odd_out], 1)
        edges = (
            row(rows_c - 1) * (-1.0 / 16.0),
            row(0) * (-1.0 / 16.0),
            (9.0 * row(0) - row(1)) * (1.0 / 16.0),
        )
        table = (xt[0], xt[1])

        def emit(block, first_row):
            high, low = halves(block)
            out = mm3(table, (high, low), NT)
            for j in range(plan.j):
                for g in range(out.shape[1] // LANES):
                    send[pl.ds(first_row(g) + j, count, stride=per), :] = out[
                        j * count : (j + 1) * count, g * LANES : (g + 1) * LANES
                    ]

        for yo in range(plan.yo):
            block = jnp.concatenate(
                [
                    field[yo * GROUP + (-g) % GROUP, zo * SUB : (zo + 1) * SUB, :]
                    for zo in range(plan.zo)
                    for g in range(GROUP)
                ],
                0,
            )
            emit(block, lambda g, yo=yo: (yo * plan.zo + g) * plan.j)
        slots = [jnp.zeros((SUB, length), jnp.float32)] * GROUP
        for zo in range(plan.zo):
            for edge in range(3):
                slots[ext_slot(edge, zo)] = edges[edge][zo * SUB : (zo + 1) * SUB]
        emit(jnp.concatenate(slots, 0), lambda g: plan.main)
        number = cell[0, 0]
        plane = fy * length
        facts = (
            (a * fz + number // plane).astype(jnp.float32),
            (b * fy + lax.rem(number // length, fy)).astype(jnp.float32),
            lax.rem(number, length).astype(jnp.float32),
            offset[0, 0],
            offset[1, 0],
            offset[2, 0],
            charge[0, 0],
            width[0, 0],
        )
        lane = lax.broadcasted_iota(jnp.int32, (1, LANES), 1)
        atom = jnp.zeros((1, LANES), jnp.float32)
        for i, fact in enumerate(facts):
            atom = jnp.where(lane == i, fact, atom)
        send[pl.ds(plan.tail, count, stride=per), :] = jnp.broadcast_to(atom, (count, LANES))
        pad = jnp.zeros((1, LANES - plan.coarse), jnp.float32)
        ahead = lax.rem(b + 1, plan.ny)
        behind = lax.rem(b + plan.ny - 1, plan.ny)
        for dest in range(plan.nz):
            for zz in range(2):
                p = lax.rem(own * dest + plan.coarse - 1 + 2 * a + zz, plan.coarse)
                for edge, target, slot in ((rows_c - 1, ahead, 0), (0, behind, 0), (1, behind, 2)):
                    line = jnp.concatenate([pad, coarse[p, edge : edge + 1, :]], 1)
                    index = slot + zz
                    if index == 0:
                        line = jnp.where(lane < SUB, atom, line)
                    send[pl.ds((dest * plan.ny + target) * per + plan.tail + index, 1), :] = line

    smem = pl.BlockSpec(memory_space=pltpu.SMEM)
    vmem = pl.BlockSpec(memory_space=pltpu.VMEM)
    return pl.pallas_call(
        kernel,
        name="spread",
        in_specs=[smem] * 4 + [vmem] * 5,
        out_specs=[vmem, vmem],
        out_shape=[
            jax.ShapeDtypeStruct((count * per, LANES), jnp.float32),
            jax.ShapeDtypeStruct((fz, fy * length), jnp.float32),
        ],
        scratch_shapes=[
            pltpu.VMEM((GROUP * rows_c, plan.coarse), jnp.float32),
            pltpu.VMEM((rows_c, fz, length), jnp.float32),
            pltpu.VMEM((fy, fz, length), jnp.float32),
        ],
        cost_estimate=pl.CostEstimate(flops=500_000_000, bytes_accessed=4_000_000, transcendentals=0),
    )


def wrapped(distance, length):
    half = length // 2
    distance = jnp.where(distance >= half, distance - length, distance)
    return jnp.where(distance < -half, distance + length, distance)


def part_b(plan):
    length, count, ext = plan.length, plan.count, plan.ext
    per, per_back = plan.rows_out, plan.rows_back

    def kernel(window, recv, zt, zti, yt, yti, lanes, wave, wave_c, send, main, shared, atoms_v, atoms, sem):
        device = lax.axis_index("gz") * plan.ny + lax.axis_index("gy")
        atoms_v[...] = recv[pl.ds(plan.tail, count, stride=per), :]
        copy = pltpu.make_async_copy(atoms_v, atoms, sem)
        copy.start()
        masks = tile_masks()
        group = masks[1]
        for j in range(plan.j):
            main[j, :SUB, :] = jnp.zeros((SUB, LANES), jnp.float32)
            main[j, SUB + length :, :] = jnp.zeros((ext - SUB - length, LANES), jnp.float32)
        for jp in range(plan.j // 2):
            shared[jp, :SUB, :] = jnp.zeros((SUB, LANES), jnp.float32)
            shared[jp, SUB + length :, :] = jnp.zeros((ext - SUB - length, LANES), jnp.float32)
        stride = plan.ny * per

        def gather(step, carry):
            jp = step // plan.ny
            b = lax.rem(step, plan.ny)
            edge_ahead = lax.rem(b + 1, plan.ny) * per
            edge_behind = lax.rem(b + plan.ny - 1, plan.ny) * per
            edges = []
            for source in (edge_behind, edge_ahead):
                edges.append(
                    [recv[pl.ds(source + plan.main + 2 * jp + k, SUB, stride=stride), :] for k in (0, 1)]
                )
            for yo in range(plan.yo):
                tiles = []
                for k in (0, 1):
                    for zo in range(plan.zo):
                        start = b * per + (yo * plan.zo + zo) * plan.j + 2 * jp + k
                        tile = recv[pl.ds(start, SUB, stride=stride), :]
                        shift = (LANES - 5 * zo * SUB) % LANES
                        if yo == 0:
                            extra = pltpu.roll(edges[0][k], shift, 1) if shift else edges[0][k]
                            tile = jnp.where(group == 15, tile + extra, tile)
                        if yo == plan.yo - 1:
                            extra = pltpu.roll(edges[1][k], shift, 1) if shift else edges[1][k]
                            tile = jnp.where((group == 3) | (group == 1), tile + extra, tile)
                        tiles.append(tile)
                at = pl.multiple_of(SUB + b * plan.fy + yo * GROUP, SUB)
                for k in (0, 1):
                    upper, lower = block_turn(tiles[3 * k], tiles[3 * k + 1], masks)
                    main[2 * jp + k, pl.ds(at, SUB), :] = upper
                    main[2 * jp + k, pl.ds(at + SUB, SUB), :] = lower
                upper, lower = block_turn(tiles[2], tiles[5], masks)
                shared[jp, pl.ds(at, SUB), :] = upper
                shared[jp, pl.ds(at + SUB, SUB), :] = lower
            return carry

        lax.fori_loop(0, plan.ny * (plan.j // 2), gather, 0)
        copy.wait()
        z_main, z_shared = lanes[0:1, :], lanes[1:2, :]
        odd = lanes[2:3, :] > 0.5
        window_rows = lax.broadcasted_iota(jnp.int32, (GROUP, LANES), 0).astype(jnp.float32) - RC

        def deposit(i, carry):
            z0, y0, x0 = atoms[i, 0], atoms[i, 1], atoms[i, 2]
            off_z, off_y, off_x = atoms[i, 3], atoms[i, 4], atoms[i, 5]
            charge, width = atoms[i, 6], atoms[i, 7]
            ratio = jnp.full((SUB, LANES), width / jnp.pi, jnp.float32)
            factor = ratio * jnp.sqrt(ratio) * charge
            factor = factor[0:1]
            cut = jnp.exp(jnp.full((SUB, LANES), -width * float(RC * RC), jnp.float32))[0:1]
            profile_y = jnp.exp(-width * (window_rows - off_y) ** 2)
            profile_x = jnp.exp(-width * (window_rows - off_x) ** 2)
            planes = []
            for z in (z_main, z_shared):
                profile_z = jnp.exp(-width * (wrapped(z - z0, length) - off_z) ** 2)
                planes.append(profile_y * profile_z)
            base = (x0.astype(jnp.int32) - RC + SUB) * SUB
            zero = jnp.zeros((GROUP, LANES), jnp.float32)
            sums = [[zero, zero, zero] for _ in range(plan.j // 2)]
            for dx in range(2 * RC + 2):
                line = profile_x[dx : dx + 1]
                bell = [jnp.maximum(plane * line - cut, 0.0) for plane in planes]
                for jp in range(plan.j // 2):
                    even = window[0, base + dx * SUB + 2 * jp]
                    odd_value = window[0, base + dx * SUB + 2 * jp + 1]
                    sums[jp][0] += bell[0] * even
                    sums[jp][1] += bell[0] * odd_value
                    sums[jp][2] += bell[1] * jnp.where(odd, odd_value, even)
            at = y0.astype(jnp.int32) - RC + SUB
            for jp in range(plan.j // 2):
                for k in (0, 1):
                    main[2 * jp + k, pl.ds(at, GROUP), :] += sums[jp][k] * factor
                shared[jp, pl.ds(at, GROUP), :] += sums[jp][2] * factor
            return carry

        lax.fori_loop(0, count, deposit, 0)
        scale = float(length) ** 2 / math.pi
        wave_y = wave_c[...][:, 0:1]
        wave_z = wave[0, 0:1, :]
        for jp in range(plan.j // 2):
            shared_back = None
            for k in (0, 1):
                j = 2 * jp + k
                left = halves(jnp.concatenate([main[j], shared[jp]], 1))
                rows_z = halves(mm3(left, (zt[0, k], zt[1, k])))
                full = mm3((yt[0], yt[1]), rows_z)
                p = j * count + device
                wave_x = jnp.where(p <= length // 2, p, p - length // 2).astype(jnp.float32)
                squares = wave_y + (wave_z + wave_x * wave_x)
                weight = jnp.where(squares > 0.0, scale / jnp.maximum(squares, 1.0), 0.0)
                weighted = halves(full * weight)
                rows_y = halves(mm3((yti[0], yti[1]), weighted))
                back = mm3(rows_y, (zti[0, k], zti[1, k]))
                main[j, SUB : SUB + length, :] = back[:, :LANES]
                part = back[:, LANES:]
                shared_back = part if shared_back is None else shared_back + part
            shared[jp, SUB : SUB + length, :] = shared_back
        stride_back = plan.ny * per_back

        def scatter(step, carry):
            jp = step // plan.ny
            b = lax.rem(step, plan.ny)
            for yo in range(plan.yo):
                at = pl.multiple_of(SUB + b * plan.fy + yo * GROUP, SUB)
                tiles = []
                for k in (0, 1):
                    tiles.append(
                        block_turn(
                            main[2 * jp + k, pl.ds(at, SUB), :],
                            main[2 * jp + k, pl.ds(at + SUB, SUB), :],
                            masks,
                        )
                    )
                both = block_turn(
                    shared[jp, pl.ds(at, SUB), :], shared[jp, pl.ds(at + SUB, SUB), :], masks
                )
                for k in (0, 1):
                    for zo, tile in enumerate((tiles[k][0], tiles[k][1], both[k])):
                        start = b * per_back + (yo * plan.zo + zo) * plan.j + 2 * jp + k
                        send[pl.ds(start, SUB, stride=stride_back), :] = tile
            return carry

        lax.fori_loop(0, plan.ny * (plan.j // 2), scatter, 0)

    smem = pl.BlockSpec(memory_space=pltpu.SMEM)
    vmem = pl.BlockSpec(memory_space=pltpu.VMEM)
    return pl.pallas_call(
        kernel,
        name="solve",
        in_specs=[smem] + [vmem] * 8,
        out_specs=vmem,
        out_shape=jax.ShapeDtypeStruct((count * per_back, LANES), jnp.float32),
        scratch_shapes=[
            pltpu.VMEM((plan.j, ext, LANES), jnp.float32),
            pltpu.VMEM((plan.j // 2, ext, LANES), jnp.float32),
            pltpu.VMEM((count, LANES), jnp.float32),
            pltpu.SMEM((count, LANES), jnp.float32),
            pltpu.SemaphoreType.DMA,
        ],
        cost_estimate=pl.CostEstimate(flops=2_000_000_000, bytes_accessed=4_000_000, transcendentals=0),
    )


def part_r(plan):
    length, fz, fy, count = plan.length, plan.fz, plan.fy, plan.count
    per = plan.rows_out

    def kernel(recv, partial, fine, kron, out, field, lines, atoms_v, atoms, sem):
        a = lax.axis_index("gz")
        b = lax.axis_index("gy")
        atoms_v[...] = recv[pl.ds(plan.tail, count, stride=per), :]
        copy = pltpu.make_async_copy(atoms_v, atoms, sem)
        copy.start()
        ahead = lax.rem(b + 1, plan.ny)
        behind = lax.rem(b + plan.ny - 1, plan.ny)
        lines[...] = jnp.zeros_like(lines)
        for source in range(plan.nz):
            for zz in range(2):
                for slot, (origin, index) in enumerate(((behind, 0), (ahead, 0), (ahead, 2))):
                    at = (source * plan.ny + origin) * per + plan.tail + index + zz
                    lines[pl.ds(slot * GROUP + 2 * source + zz, 1), :] = recv[pl.ds(at, 1), :]
        block = lines[...][:, LANES - plan.coarse :]
        wide = sum(mm(piece, fine[...], NN) for piece in thirds(block)[::-1])
        tall = sum(mm(kron[...], piece, NN) for piece in thirds(wide)[::-1])
        below, above, above2 = (tall[i * fz : (i + 1) * fz] for i in range(3))
        field[...] = jnp.zeros_like(field)
        field[1] = below * (-1.0 / 16.0)
        field[fy - 3] = above * (-1.0 / 16.0)
        field[fy - 1] = (9.0 * above - above2) * (1.0 / 16.0)
        copy.wait()
        z_here = lax.broadcasted_iota(jnp.int32, (fz, length), 0).astype(jnp.float32)
        x_here = lax.broadcasted_iota(jnp.int32, (fz, length), 1).astype(jnp.float32)

        def deposit(i, carry):
            z0 = wrapped(atoms[i, 0] - (a * fz).astype(jnp.float32), length)
            y0 = wrapped(atoms[i, 1] - (b * fy).astype(jnp.float32), length).astype(jnp.int32)
            first = jnp.maximum(y0 - RC, 0)
            last = jnp.minimum(y0 + RC + 2, fy)
            near_z = (z0 > -RC - 2.0) & (z0 < fz + RC + 1.0)

            @pl.when(near_z & (first < last))
            def _():
                off_z, off_y, off_x = atoms[i, 3], atoms[i, 4], atoms[i, 5]
                charge, width = atoms[i, 6], atoms[i, 7]
                ratio = jnp.full((fz, length), width / jnp.pi, jnp.float32)
                factor = ratio * jnp.sqrt(ratio) * charge
                cut = jnp.exp(jnp.full((fz, length), -width * float(RC * RC), jnp.float32))
                dist_z = z_here - z0 - off_z
                dist_x = wrapped(x_here - atoms[i, 2], length) - off_x
                flat = dist_z * dist_z + dist_x * dist_x

                def row(y, inner):
                    dist_y = (y - y0).astype(jnp.float32) - off_y
                    bell = jnp.maximum(jnp.exp(-width * (flat + dist_y * dist_y)) - cut, 0.0)
                    field[y] += bell * factor
                    return inner

                lax.fori_loop(first, last, row, 0)

            return carry

        lax.fori_loop(0, count, deposit, 0)
        for i in range(fy // 2):
            span = slice(2 * i * length, (2 * i + 2) * length)
            out[:, span] = partial[:, span] + jnp.concatenate([field[2 * i], field[2 * i + 1]], 1)

    vmem = pl.BlockSpec(memory_space=pltpu.VMEM)
    return pl.pallas_call(
        kernel,
        name="finish",
        in_specs=[vmem] * 4,
        out_specs=vmem,
        out_shape=jax.ShapeDtypeStruct((fz, fy * length), jnp.float32),
        scratch_shapes=[
            pltpu.VMEM((fy, fz, length), jnp.float32),
            pltpu.VMEM((SUB * GROUP, LANES), jnp.float32),
            pltpu.VMEM((count, LANES), jnp.float32),
            pltpu.SMEM((count, LANES), jnp.float32),
            pltpu.SemaphoreType.DMA,
        ],
        cost_estimate=pl.CostEstimate(flops=3_000_000_000, bytes_accessed=4_000_000, transcendentals=0),
    )


def part_c(plan, terms):
    length, fz, fy, count = plan.length, plan.fz, plan.fy, plan.count
    per = plan.rows_back
    span = GROUP * length

    def kernel(recv, xt, history, residual, potential, sums, acc):
        step = pl.program_id(0)
        pieces = []
        for zo in range(plan.zo):
            spectrum = jnp.concatenate(
                [
                    recv[pl.ds((step * plan.zo + zo) * plan.j + j, count, stride=per), :]
                    for j in range(plan.j)
                ],
                0,
            )
            pieces.append(spectrum.T)
        values = mm3(halves(jnp.concatenate(pieces, 0)), (xt[0], xt[1]))
        for pair in range(GROUP // 2):
            for zo in range(plan.zo):
                at = zo * LANES + 2 * pair * SUB
                potential[zo * SUB : (zo + 1) * SUB, 2 * pair * length : (2 * pair + 2) * length] = (
                    jnp.concatenate([values[at : at + SUB], values[at + SUB : at + 2 * SUB]], 1)
                )

        @pl.when(step == 0)
        def _():
            acc[...] = jnp.zeros_like(acc)

        wide = 3 * LANES
        for i in range(terms + 1):
            total = jnp.zeros((fz, wide), jnp.float32)
            for c in range(span // wide):
                cut = slice(c * wide, (c + 1) * wide)
                other = history[i, :, cut] if i < terms else residual[:, cut]
                total += other * potential[:, cut]
            acc[i * SUB : (i + 1) * SUB, :] += sum(
                total[r * SUB : (r + 1) * SUB, q * LANES : (q + 1) * LANES]
                for r in range(plan.zo)
                for q in range(3)
            )

        @pl.when(step == pl.num_programs(0) - 1)
        def _():
            lane = lax.broadcasted_iota(jnp.int32, (1, LANES), 1)
            line = jnp.zeros((1, LANES), jnp.float32)
            for i in range(terms + 1):
                line = jnp.where(lane == i, jnp.sum(acc[i * SUB : (i + 1) * SUB, :]), line)
            sums[...] = jnp.broadcast_to(line * (1.0 / float(length) ** 3), (count, LANES))

    return pl.pallas_call(
        kernel,
        name="finish_potential",
        grid=(plan.yo,),
        in_specs=[
            pl.BlockSpec((count * per, LANES), lambda s: (0, 0)),
            pl.BlockSpec((2, length, length), lambda s: (0, 0, 0)),
            pl.BlockSpec((terms, fz, span), lambda s: (0, 0, s)),
            pl.BlockSpec((fz, span), lambda s: (0, s)),
        ],
        out_specs=[
            pl.BlockSpec((fz, span), lambda s: (0, s)),
            pl.BlockSpec((count, LANES), lambda s: (0, 0)),
        ],
        out_shape=[
            jax.ShapeDtypeStruct((fz, fy * length), jnp.float32),
            jax.ShapeDtypeStruct((count, LANES), jnp.float32),
        ],
        scratch_shapes=[pltpu.VMEM(((terms + 1) * SUB, LANES), jnp.float32)],
        compiler_params=pltpu.CompilerParams(dimension_semantics=("arbitrary",)),
        cost_estimate=pl.CostEstimate(flops=500_000_000, bytes_accessed=10_000_000, transcendentals=0),
    )


def exchange(sent, count, axes):
    blocks = sent.reshape(count, sent.shape[0] // count, LANES)
    return lax.all_to_all(blocks, axes, 0, 0, tiled=True).reshape(sent.shape)


def local_fast(plan, coarse_density, density_in, history, atom_cell, atom_offset, atom_charge, atom_width):
    axes = ("gz", "gy")
    count = plan.count
    tables_ = fast_tables(plan)
    sent, partial = part_a(plan)(
        atom_cell.reshape(1, 1),
        atom_offset.reshape(3, 1),
        atom_charge.reshape(1, 1),
        atom_width.reshape(1, 1),
        coarse_density,
        density_in,
        tables_["fine"],
        tables_["kron"],
        tables_["x"],
    )
    spectra = exchange(sent, count, axes)
    device = lax.axis_index("gz") * plan.ny + lax.axis_index("gy")
    window = lax.dynamic_slice_in_dim(tables_["window"], device, 1, 0)
    solved = part_b(plan)(
        window,
        spectra,
        tables_["z"],
        tables_["zt"],
        tables_["y"],
        tables_["yt"],
        tables_["lanes"],
        tables_["wave"],
        tables_["wave_c"],
    )
    back = exchange(solved, count, axes)
    residual = part_r(plan)(spectra, partial, tables_["fine"], tables_["kron"])
    potential, sums = part_c(plan, history.shape[0])(back, tables_["x"], history, residual)
    rows = lax.all_to_all(sums, axes, 0, 0, tiled=True)
    return residual, potential, jnp.sum(rows, 0)[: history.shape[0] + 1]


def solution(mesh):
    in_specs = (
        P(None, "gy", None),
        P("gz", "gy"),
        P(None, "gz", "gy"),
        P("gz", "gy", None),
        P(None, "gz", "gy", None),
        P("gz", "gy", None),
        P("gz", "gy", None),
    )
    out_specs = (P("gz", "gy"), P("gz", "gy"), P())

    def body(*arguments):
        coarse_density, density_in = arguments[:2]
        plan = Plan(
            (mesh.shape["gz"], mesh.shape["gy"]),
            2 * coarse_density.shape[0],
            coarse_density.shape[0],
            density_in.shape[0],
            2 * coarse_density.shape[1],
        )
        if plan.ok():
            return local_fast(plan, *arguments)
        return local(*arguments)

    return jax.shard_map(body, mesh=mesh, in_specs=in_specs, out_specs=out_specs, check_vma=False)
```

profile of v0, /device:TPU:0, one launch (start us, length us, event | category | flops | bytes accessed | tf_op | source)
XLA Modules:
  0.0 104.7 jit_solution(8756781028325424760)
XLA Ops:
  1.3 1.3 %copy.22.offset = f32[3,1]{1,0:T(4,128)} copy(f32[3,1]{0,1:T(1,128)} %bitcast.21) | data formatting | bytes 24 | tf_op jit(solution)/shard_map/reshape | solution.py:815
  3.9 4.8 %spread.1 = (f32[2048,128]{1,0:T(8,128)}, f32[24,9216]{1,0:T(8,128)}) custom-call(s32[1,1]{1,0:T(1,128)} %bitcast.12.cell, f32[3,1]{1,0:T(4,128)} %copy.22.offset, f32[1,1]{1,0:T(1,128)} %bitcast.13.charge, f32[1,1]{1,0:T(1,128)} %bitcast.14.width, f32[96,24,96]{2,1,0:T(8,128)} %coarse.1, f32[24,9216]{1,0:T(8,128)} %density.1, ...), custom_call_target="tpu_custom_call" | custom-call | flops 500000000 | bytes 4000000 | tf_op jit(solution)/shard_map/spread/pallas_call | solution.py:813
  8.7 7.3 %all-to-all-start = ((f32[32,64,128]{2,1,0:T(8,128)}), f32[32,64,128]{2,1,0:T(8,128)S(1)}, u32[]{:S(2)}, u32[]{:S(2)}) async-start(f32[32,64,128]{2,1,0:T(8,128)} %bitcast.18), calls=%async_computation | async-start | bytes 2097152 | tf_op jit(solution)/shard_map/all_to_all | solution.py:806
  16.1 1.4 %constant_dynamic-slice_fusion.window = f32[1,1664]{1,0:T(1,128)} fusion(f32[32,1664]{1,0:T(8,128)} %constant.49.clone, s32[]{:T(128)S(6)} %select_n.3), kind=kLoop, calls=%fused_computation | loop fusion | bytes 13316 | tf_op jit(solution)/shard_map/dynamic_slice | solution.py:826
  17.5 23.5 %all-to-all-done = f32[32,64,128]{2,1,0:T(8,128)S(1)} async-done(((f32[32,64,128]{2,1,0:T(8,128)}), f32[32,64,128]{2,1,0:T(8,128)S(1)}, u32[]{:S(2)}, u32[]{:S(2)}) %all-to-all-start) | async-done | bytes 1048608 | tf_op jit(solution)/shard_map/all_to_all | solution.py:806
  41.0 0.0 copy-start.1
  41.0 1.4 %jit_solution_.3.wave_c = f32[192,128]{1,0:T(8,128)} broadcast(f32[192]{0:T(256)} %constant.48.clone), dimensions={0} | broadcast | bytes 99072 | tf_op jit(solution)
  42.4 0.0 copy-done.1
  42.4 16.1 %solve.1 = f32[1792,128]{1,0:T(8,128)} custom-call(f32[1,1664]{1,0:T(1,128)} %constant_dynamic-slice_fusion.window, f32[2048,128]{1,0:T(8,128)} %bitcast.16, bf16[2,2,256,192]{3,2,1,0:T(8,128)(2,1)} %constant.42.clone.zt, bf16[2,2,192,256]{3,2,1,0:T(8,128)(2,1)} %constant.43.clone.zti, bf16[2,192,216]{2,1,0:T(8,128)(2,1)} %constant.44.clone.yt, ...), custom_call_target="tpu_custom_call" | custom-call | flops 2000000000 | bytes 4000000 | tf_op jit(solution)/shard_map/solve/pallas_call | solution.py:827
  58.5 4.6 %all-to-all-start.1 = ((f32[32,56,128]{2,1,0:T(8,128)}), f32[32,56,128]{2,1,0:T(8,128)S(1)}, u32[]{:S(2)}, u32[]{:S(2)}) async-start(f32[32,56,128]{2,1,0:T(8,128)} %bitcast.19), calls=%async_computation.1 | async-start | bytes 1835008 | tf_op jit(solution)/shard_map/all_to_all | solution.py:806
  63.1 5.0 %finish.1.residual = f32[24,9216]{1,0:T(8,128)} custom-call(f32[2048,128]{1,0:T(8,128)} %bitcast.17, f32[24,9216]{1,0:T(8,128)} %get-tuple-element.8.partial, bf16[96,192]{1,0:T(8,128)(2,1)} %constant.40.clone.fine, bf16[192,128]{1,0:T(8,128)(2,1)} %constant.41.clone.kron), custom_call_target="tpu_custom_call" | custom-call | flops 3000000000 | bytes 4000000 | tf_op jit(solution)/shard_map/finish/pallas_call | solution.py:839
  68.1 17.2 %all-to-all-done.1 = f32[32,56,128]{2,1,0:T(8,128)S(1)} async-done(((f32[32,56,128]{2,1,0:T(8,128)}), f32[32,56,128]{2,1,0:T(8,128)S(1)}, u32[]{:S(2)}, u32[]{:S(2)}) %all-to-all-start.1) | async-done | bytes 917536 | tf_op jit(solution)/shard_map/all_to_all | solution.py:806
  85.3 0.0 copy-start
  85.3 0.9 copy-done
  86.2 6.2 %finish_potential.1 = (f32[24,9216]{1,0:T(8,128)}, f32[32,128]{1,0:T(8,128)}) custom-call(f32[1792,128]{1,0:T(8,128)} %bitcast.15, bf16[2,192,192]{2,1,0:T(8,128)(2,1)} %constant.39.clone.xt, f32[8,24,9216]{2,1,0:T(8,128)} %history.1, f32[24,9216]{1,0:T(8,128)} %finish.1.residual), custom_call_target="tpu_custom_call" | custom-call | flops 500000000 | bytes 10000000 | tf_op jit(solution)/shard_map/finish_potential/pallas_call | solution.py:840
  92.4 11.7 %all_to_all.19 = f32[32,1,128]{2,1,0:T(1,128)S(1)} all-to-all(f32[32,1,128]{2,1,0:T(1,128)} %bitcast.20), channel_id=1, replica_groups=mesh['gz'=8,'gy'=4] {'gz','gy'}, dimensions={0} | all-to-all | bytes 32768 | tf_op jit(solution)/shard_map/all_to_all | solution.py:841
  104.1 0.6 reduce_sum.9
Async XLA Ops:
  8.7 32.3 %all-to-all-start = ((f32[32,64,128]{2,1,0:T(8,128)}), f32[32,64,128]{2,1,0:T(8,128)S(1)}, u32[]{:S(2)}, u32[]{:S(2)}) async-start(f32[32,64,128]{2,1,0:T(8,128)} %bitcast.18), calls=%async_computation | async-start | bytes 2097152 | tf_op jit(solution)/shard_map/all_to_all | solution.py:806
  41.0 1.4 %copy-start.1 = (f32[32,64,128]{2,1,0:T(8,128)}, f32[32,64,128]{2,1,0:T(8,128)S(1)}, u32[]{:S(2)}) copy-start(f32[32,64,128]{2,1,0:T(8,128)S(1)} %all-to-all-done) | copy-start | bytes 3145732
  58.5 26.8 %all-to-all-start.1 = ((f32[32,56,128]{2,1,0:T(8,128)}), f32[32,56,128]{2,1,0:T(8,128)S(1)}, u32[]{:S(2)}, u32[]{:S(2)}) async-start(f32[32,56,128]{2,1,0:T(8,128)} %bitcast.19), calls=%async_computation.1 | async-start | bytes 1835008 | tf_op jit(solution)/shard_map/all_to_all | solution.py:806
  85.3 0.9 copy-start
where the time goes:
time: 105 us
  waiting for transfers between devices  40.7 us (39%)
  Pallas kernels  32.1 us (31%)
  starting transfers between devices  11.9 us (11%)
  blocking collectives  11.7 us (11%)
  local copies, waits for them, and re-layouts  5.08 us (5%)
  between operations  2.62 us (2%)
    all_to_all x2, waiting for transfers between devices, exchange(): return lax.all_to_all(blocks, axes, 0, 0, tiled=True).reshape(sent.shape)  40.7 us
    pallas_call x1, Pallas kernels, local_fast(): part_b(plan)  16.1 us
    all_to_all x2, starting transfers between devices, exchange(): return lax.all_to_all(blocks, axes, 0, 0, tiled=True).reshape(sent.shape)  11.9 us
    all_to_all x1, blocking collectives, local_fast(): rows = lax.all_to_all(sums, axes, 0, 0, tiled=True)  11.7 us
    pallas_call x1, Pallas kernels, local_fast(): part_c(plan, history.shape[0])(back, tables_['x'], history, residual)  6.15 us
    pallas_call x1, Pallas kernels, local_fast(): residual = part_r(plan)(spectra, partial, tables_['fine'], tables_['kron'])  4.98 us
    pallas_call x1, Pallas kernels, local_fast(): part_a(plan)  4.85 us
  transfers between devices with their start and end apart: 2, of which 2 were waited for; matrix products, arithmetic and copies ran while one was open for 1% of the time, Pallas kernels for 5%

commit v1 on v0

--- a/solution.py
+++ b/solution.py
@@ -224,13 +224,6 @@
     return rows * scale[:, None], wave
 
 
-def split_table(table):
-    table = np.asarray(table, np.float32)
-    high = table.astype(jnp.bfloat16)
-    low = (table - high.astype(np.float32)).astype(jnp.bfloat16)
-    return jnp.asarray(np.stack([high, low]))
-
-
 def halves(values):
     high = values.astype(jnp.bfloat16)
     return high, (values - high.astype(jnp.float32)).astype(jnp.bfloat16)
@@ -252,9 +245,48 @@
 
 
 def mm3(left, right, dims=NN):
-    return (
-        mm(left[0], right[1], dims) + mm(left[1], right[0], dims) + mm(left[0], right[0], dims)
-    )
+    rows = left[0].shape[0]
+    both = mm(jnp.concatenate(left, 0), right[0], dims)
+    return mm(left[0], right[1], dims) + both[rows:] + both[:rows]
+
+
+def turn_tiles(tiles):
+    row = lax.broadcasted_iota(jnp.int32, (SUB, LANES), 0)
+    tiles = list(tiles)
+    for step in (4, 2, 1):
+        own = (row & step) == 0
+        for i in range(SUB):
+            if i & step == 0:
+                first, second = tiles[i], tiles[i + step]
+                tiles[i] = jnp.where(own, first, pltpu.roll(second, step, 0))
+                tiles[i + step] = jnp.where(own, pltpu.roll(first, SUB - step, 0), second)
+    return tiles
+
+
+def slot(g, pair, k):
+    if g < 7:
+        return SUB * g + 2 * pair + k
+    return SUB * (3 * (g - 7) + pair) + 6 + k
+
+
+def fetch(pairs, sems, first=0):
+    copies = [
+        pltpu.make_async_copy(source, target, sems.at[first + i])
+        for i, (source, target) in enumerate(pairs)
+    ]
+    for copy in copies:
+        copy.start()
+    return copies
+
+
+def room(array):
+    return pltpu.VMEM(array.shape, array.dtype)
+
+
+TAIL = (54, 55, 62, 63)
+EDGE = 56
+VMEM_LIMIT = 60 * 1024 * 1024
+LATE_LIMIT = 48 * 1024 * 1024
 
 
 def tile_masks():
@@ -294,11 +326,9 @@
         self.length, self.coarse, self.fz, self.fy = length, coarse, fz, fy
         self.j = length // self.count
         self.zo, self.yo = fz // SUB, fy // GROUP
-        self.main = self.j * self.zo * self.yo
-        self.tail = self.main + self.j
-        self.rows_out = self.tail + 4
-        self.rows_back = -(-self.main // SUB) * SUB
-        self.ext = length + 24
+        self.rows_out = 64
+        self.rows_back = 56
+        self.ext = length + 32
 
     def ok(self):
         return (
@@ -306,7 +336,6 @@
             and self.fz % SUB == 0
             and self.fy % GROUP == 0
             and self.length == self.coarse * 2
-            and self.rows_out % SUB == 0
         )
 
 
@@ -340,40 +369,78 @@
             table[:LANES] = rows[:, z_main].T
             table[LANES:] = np.where((odd == parity)[:, None], rows[:, z_shared].T, 0.0)
             tables_z.append(table)
-        return tables_z, (z_main, z_shared, odd)
-
-    z_tables, z_lanes = along_z(np.arange(GROUP))
-    z_back = along_z((-np.arange(GROUP)) % GROUP)[0]
+        return tables_z
+
+    z_tables = along_z(np.arange(GROUP))
+    z_back = along_z((-np.arange(GROUP)) % GROUP)
     y_of_row = (np.arange(plan.ext) - SUB) % length
-    lanes = np.zeros((SUB, LANES), np.float32)
-    lanes[0], lanes[1], lanes[2] = z_lanes
-    squares = (wave.astype(np.float64) ** 2).astype(np.float32)
-    x_window = np.zeros((plan.count, length + GROUP, SUB), np.float32)
+    count = plan.count
+    x_window = np.zeros((count, length + GROUP, SUB), np.float32)
     x_of_row = (np.arange(length + GROUP) - SUB) % length
-    for d in range(plan.count):
+    padded = np.zeros((count, SUB, length))
+    kept = np.zeros((count, SUB, length))
+    donors = np.zeros((3, count, SUB, length))
+    for d in range(count):
         for j in range(plan.j):
-            x_window[d, :, j] = rows[j * plan.count + d, x_of_row]
+            mode = rows[j * count + d]
+            x_window[d, :, j] = mode[x_of_row]
+            padded[d, j] = kept[d, j] = mode
+            donors[j // 2, d, 6 + j % 2] = mode
+        padded[d, 6:] = padded[d, 4:6]
+    flat = lambda table: table.reshape(count * SUB, length)
+    def halves_of(table):
+        table = np.asarray(table, np.float32)
+        high = table.astype(jnp.bfloat16)
+        return [high, (table - high.astype(np.float32)).astype(jnp.bfloat16)]
+
+    def pack(tables_in):
+        width = max(table.shape[-1] for table in tables_in)
+        return jnp.asarray(
+            np.concatenate(
+                [
+                    np.pad(table, ((0, 0), (0, width - table.shape[-1])))
+                    for table in tables_in
+                ],
+                0,
+            )
+        )
+
+    z_all = np.stack(z_tables).reshape(-1, length)
+    zt_all = np.stack([t.T for t in z_back]).reshape(-1, 2 * LANES)
+    near = [np.kron(np.eye(SUB), local_z), fine_of]
     return {
-        "x": split_table(rows),
-        "fine": jnp.asarray(fine_of, jnp.bfloat16),
-        "kron": jnp.asarray(np.kron(np.eye(SUB), local_z), jnp.bfloat16),
-        "z": split_table(np.stack(z_tables)),
-        "zt": split_table(np.stack([t.T for t in z_back])),
-        "y": split_table(rows[:, y_of_row]),
-        "yt": split_table(rows.T),
-        "lanes": jnp.asarray(lanes),
-        "wave": jnp.asarray(np.stack([np.broadcast_to(squares, (SUB, length))])),
-        "wave_c": jnp.asarray(np.broadcast_to(squares[:, None], (length, LANES))),
-        "window": jnp.asarray(x_window.reshape(plan.count, -1)),
+        "a": pack(halves_of(flat(padded)) + [table.astype(jnp.bfloat16) for table in near]),
+        "b": pack(
+            halves_of(z_all) + halves_of(zt_all) + halves_of(rows[:, y_of_row]) + halves_of(rows.T)
+        ),
+        "c": pack(halves_of(np.stack([flat(kept)] + [flat(donors[i]) for i in range(3)]).reshape(-1, length))),
+        "window": jnp.asarray(x_window.reshape(count, 1, -1)),
     }
 
 
-def part_a(plan):
+def near_tables(plan, near, first):
+    kron_rows = SUB * plan.fz
+    kron = near[first : first + kron_rows, :LANES]
+    return kron, near[first + kron_rows : first + kron_rows + plan.coarse, :]
+
+
+def part_a(plan, t):
     length, fz, fy, count = plan.length, plan.fz, plan.fy, plan.count
     rows_c = fy // 2
     per = plan.rows_out
 
-    def kernel(cell, offset, charge, width, coarse, density, fine, kron, xt, send, partial, planes, smooth, field):
+    def kernel(
+        cell_h, offset_h, charge_h, width_h, coarse_h, density_h, table_h, send_h, partial_h,
+        cell, offset, charge, width, coarse, density, tables_v, send, partial, planes, smooth, field, donor, sems,
+    ):
+        first = fetch([(coarse_h, coarse), (table_h, tables_v)], sems)
+        second = fetch([(density_h, density)], sems, 3)
+        facts_in = fetch(
+            [(cell_h, cell), (offset_h, offset), (charge_h, charge), (width_h, width)], sems, 4
+        )
+        for copy in first:
+            copy.wait()
+        kron, fine = near_tables(plan, tables_v, 2 * count * SUB)
         a = lax.axis_index("gz")
         b = lax.axis_index("gy")
         own = plan.coarse // plan.nz
@@ -383,14 +450,15 @@
             block = jnp.concatenate(
                 [planes[pl.ds(part * SUB + y, GROUP, stride=rows_c), :] for y in range(SUB)], 0
             )
-            wide = sum(mm(piece, fine[...], NN) for piece in thirds(block)[::-1])
-            tall = sum(mm(kron[...], piece, NN) for piece in thirds(wide)[::-1])
+            wide = sum(mm(piece, fine, NN) for piece in thirds(block)[::-1])
+            tall = sum(mm(kron, piece, NN) for piece in thirds(wide)[::-1])
             for y in range(SUB):
                 smooth[part * SUB + y] = tall[y * fz : (y + 1) * fz]
 
         def row(i):
             return smooth[i] if 0 <= i < rows_c else jnp.zeros((fz, length), jnp.float32)
 
+        second[0].wait()
         for i in range(rows_c):
             odd_row = (9.0 * (row(i) + row(i + 1)) - row(i - 1) - row(i + 2)) * (1.0 / 16.0)
             old = density[:, 2 * i * length : (2 * i + 2) * length]
@@ -404,18 +472,18 @@
             row(0) * (-1.0 / 16.0),
             (9.0 * row(0) - row(1)) * (1.0 / 16.0),
         )
-        table = (xt[0], xt[1])
-
-        def emit(block, first_row):
-            high, low = halves(block)
-            out = mm3(table, (high, low), NT)
-            for j in range(plan.j):
-                for g in range(out.shape[1] // LANES):
-                    send[pl.ds(first_row(g) + j, count, stride=per), :] = out[
-                        j * count : (j + 1) * count, g * LANES : (g + 1) * LANES
-                    ]
-
-        for yo in range(plan.yo):
+        out_partial = fetch([(partial, partial_h)], sems, 9)
+        table = (tables_v[: count * SUB, :], tables_v[count * SUB : 2 * count * SUB, :])
+        sub_row = lax.broadcasted_iota(jnp.int32, (count, SUB, LANES), 1)
+
+        def modes(block):
+            out = mm3(table, halves(block), NT)
+            return [
+                out[:, g * LANES : (g + 1) * LANES].reshape(count, SUB, LANES)
+                for g in range(out.shape[1] // LANES)
+            ]
+
+        for yo in (2, 0, 1):
             block = jnp.concatenate(
                 [
                     field[yo * GROUP + (-g) % GROUP, zo * SUB : (zo + 1) * SUB, :]
@@ -424,29 +492,42 @@
                 ],
                 0,
             )
-            emit(block, lambda g, yo=yo: (yo * plan.zo + g) * plan.j)
+            found = modes(block)
+            if yo == 2:
+                send[:, 48:56, :] = found[0]
+                donor[0] = found[1]
+                donor[1] = found[2]
+            else:
+                for pair in range(3):
+                    other = donor[yo]
+                    if pair < 2:
+                        other = pltpu.roll(other, 6 - 2 * pair, 1)
+                    at = SUB * (3 * yo + pair)
+                    send[:, at : at + SUB, :] = jnp.where(sub_row < 6, found[pair], other)
         slots = [jnp.zeros((SUB, length), jnp.float32)] * GROUP
         for zo in range(plan.zo):
             for edge in range(3):
                 slots[ext_slot(edge, zo)] = edges[edge][zo * SUB : (zo + 1) * SUB]
-        emit(jnp.concatenate(slots, 0), lambda g: plan.main)
-        number = cell[0, 0]
+        send[:, EDGE : EDGE + SUB, :] = modes(jnp.concatenate(slots, 0))[0]
+        for copy in facts_in:
+            copy.wait()
+        number = cell[0]
         plane = fy * length
         facts = (
             (a * fz + number // plane).astype(jnp.float32),
             (b * fy + lax.rem(number // length, fy)).astype(jnp.float32),
             lax.rem(number, length).astype(jnp.float32),
-            offset[0, 0],
-            offset[1, 0],
-            offset[2, 0],
-            charge[0, 0],
-            width[0, 0],
+            offset[0],
+            offset[1],
+            offset[2],
+            charge[0],
+            width[0],
         )
         lane = lax.broadcasted_iota(jnp.int32, (1, LANES), 1)
         atom = jnp.zeros((1, LANES), jnp.float32)
         for i, fact in enumerate(facts):
             atom = jnp.where(lane == i, fact, atom)
-        send[pl.ds(plan.tail, count, stride=per), :] = jnp.broadcast_to(atom, (count, LANES))
+        send[:, TAIL[0] : TAIL[0] + 1, :] = jnp.broadcast_to(atom[None], (count, 1, LANES))
         pad = jnp.zeros((1, LANES - plan.coarse), jnp.float32)
         ahead = lax.rem(b + 1, plan.ny)
         behind = lax.rem(b + plan.ny - 1, plan.ny)
@@ -458,23 +539,37 @@
                     index = slot + zz
                     if index == 0:
                         line = jnp.where(lane < SUB, atom, line)
-                    send[pl.ds((dest * plan.ny + target) * per + plan.tail + index, 1), :] = line
-
-    smem = pl.BlockSpec(memory_space=pltpu.SMEM)
-    vmem = pl.BlockSpec(memory_space=pltpu.VMEM)
+                    send[dest * plan.ny + target, TAIL[index] : TAIL[index] + 1, :] = line
+        out_send = fetch([(send, send_h)], sems, 10)
+        for copy in out_partial + out_send:
+            copy.wait()
+
+    hbm = pl.BlockSpec(memory_space=pltpu.HBM)
     return pl.pallas_call(
         kernel,
         name="spread",
-        in_specs=[smem] * 4 + [vmem] * 5,
-        out_specs=[vmem, vmem],
+        in_specs=[hbm] * 7,
+        out_specs=[hbm, hbm],
         out_shape=[
-            jax.ShapeDtypeStruct((count * per, LANES), jnp.float32),
+            jax.ShapeDtypeStruct((count, per, LANES), jnp.float32),
             jax.ShapeDtypeStruct((fz, fy * length), jnp.float32),
         ],
+        compiler_params=pltpu.CompilerParams(vmem_limit_bytes=VMEM_LIMIT),
         scratch_shapes=[
+            pltpu.SMEM((1,), jnp.int32),
+            pltpu.SMEM((3,), jnp.float32),
+            pltpu.SMEM((1,), jnp.float32),
+            pltpu.SMEM((1,), jnp.float32),
+            pltpu.VMEM((plan.coarse, rows_c, plan.coarse), jnp.float32),
+            pltpu.VMEM((fz, fy * length), jnp.float32),
+            room(t["a"]),
+            pltpu.VMEM((count, per, LANES), jnp.float32),
+            pltpu.VMEM((fz, fy * length), jnp.float32),
             pltpu.VMEM((GROUP * rows_c, plan.coarse), jnp.float32),
             pltpu.VMEM((rows_c, fz, length), jnp.float32),
             pltpu.VMEM((fy, fz, length), jnp.float32),
+            pltpu.VMEM((2, count, SUB, LANES), jnp.float32),
+            pltpu.SemaphoreType.DMA((11,)),
         ],
         cost_estimate=pl.CostEstimate(flops=500_000_000, bytes_accessed=4_000_000, transcendentals=0),
     )
@@ -486,13 +581,43 @@
     return jnp.where(distance < -half, distance + length, distance)
 
 
-def part_b(plan):
+def part_b(plan, t):
     length, count, ext = plan.length, plan.count, plan.ext
     per, per_back = plan.rows_out, plan.rows_back
 
-    def kernel(window, recv, zt, zti, yt, yti, lanes, wave, wave_c, send, main, shared, atoms_v, atoms, sem):
+    def kernel(
+        window_h, recv_h, table_h, send_h,
+        window, recv, tables_v, send, main, shared, turned, ready, atoms_v, atoms, sem, sems, sems_in, sems_out,
+    ):
         device = lax.axis_index("gz") * plan.ny + lax.axis_index("gy")
-        atoms_v[...] = recv[pl.ds(plan.tail, count, stride=per), :]
+
+        def incoming(b):
+            return pltpu.make_async_copy(recv_h.at[:, b], recv.at[:, b], sems_in.at[b])
+
+        def outgoing(b):
+            return pltpu.make_async_copy(send.at[:, b], send_h.at[:, b], sems_out.at[b])
+
+        for b in range(plan.ny):
+            incoming(b).start()
+        copies = fetch(
+            [
+                (window_h.at[device], window),
+                (table_h, tables_v),
+            ],
+            sems,
+        )
+        def unpack(b, carry):
+            incoming(b).wait()
+            for t in range(per // SUB):
+                tiles = turn_tiles(
+                    [recv[a, b, t * SUB : (t + 1) * SUB, :] for a in range(plan.nz)]
+                )
+                for i, tile in enumerate(tiles):
+                    turned[b, t * SUB + i] = tile
+            atoms_v[pl.ds(pl.multiple_of(b * SUB, SUB), SUB), :] = turned[b, TAIL[0]]
+            return carry
+
+        lax.fori_loop(0, plan.ny, unpack, 0)
         copy = pltpu.make_async_copy(atoms_v, atoms, sem)
         copy.start()
         masks = tile_masks()
@@ -503,24 +628,19 @@
         for jp in range(plan.j // 2):
             shared[jp, :SUB, :] = jnp.zeros((SUB, LANES), jnp.float32)
             shared[jp, SUB + length :, :] = jnp.zeros((ext - SUB - length, LANES), jnp.float32)
-        stride = plan.ny * per
-
         def gather(step, carry):
             jp = step // plan.ny
             b = lax.rem(step, plan.ny)
-            edge_ahead = lax.rem(b + 1, plan.ny) * per
-            edge_behind = lax.rem(b + plan.ny - 1, plan.ny) * per
+            edge_ahead = lax.rem(b + 1, plan.ny)
+            edge_behind = lax.rem(b + plan.ny - 1, plan.ny)
             edges = []
             for source in (edge_behind, edge_ahead):
-                edges.append(
-                    [recv[pl.ds(source + plan.main + 2 * jp + k, SUB, stride=stride), :] for k in (0, 1)]
-                )
+                edges.append([turned[source, EDGE + 2 * jp + k] for k in (0, 1)])
             for yo in range(plan.yo):
                 tiles = []
                 for k in (0, 1):
                     for zo in range(plan.zo):
-                        start = b * per + (yo * plan.zo + zo) * plan.j + 2 * jp + k
-                        tile = recv[pl.ds(start, SUB, stride=stride), :]
+                        tile = turned[b, slot(yo * plan.zo + zo, jp, k)]
                         shift = (LANES - 5 * zo * SUB) % LANES
                         if yo == 0:
                             extra = pltpu.roll(edges[0][k], shift, 1) if shift else edges[0][k]
@@ -541,8 +661,14 @@
 
         lax.fori_loop(0, plan.ny * (plan.j // 2), gather, 0)
         copy.wait()
-        z_main, z_shared = lanes[0:1, :], lanes[1:2, :]
-        odd = lanes[2:3, :] > 0.5
+        for item in copies:
+            item.wait()
+        lane = lax.broadcasted_iota(jnp.int32, (1, LANES), 1)
+        block = lane // SUB
+        odd = block >= SUB
+        z_first = (block & (SUB - 1)) * plan.fz + (lane & (SUB - 1))
+        z_main = (z_first + jnp.where(odd, SUB, 0)).astype(jnp.float32)
+        z_shared = (z_first + 2 * SUB).astype(jnp.float32)
         window_rows = lax.broadcasted_iota(jnp.int32, (GROUP, LANES), 0).astype(jnp.float32) - RC
 
         def deposit(i, carry):
@@ -580,27 +706,55 @@
 
         lax.fori_loop(0, count, deposit, 0)
         scale = float(length) ** 2 / math.pi
-        wave_y = wave_c[...][:, 0:1]
-        wave_z = wave[0, 0:1, :]
+        half = length // 2
+
+        def square(mode):
+            wave = jnp.where(mode <= half, mode, mode - half)
+            return (wave * wave).astype(jnp.float32)
+
+        plane = square(lax.broadcasted_iota(jnp.int32, (length, length), 0)) + square(
+            lax.broadcasted_iota(jnp.int32, (length, length), 1)
+        )
+        zt, zti, yt, yti = [], [], [], []
+        at = 0
+        for into, size, width, parts in (
+            (zt, 2 * LANES, length, 2),
+            (zti, length, 2 * LANES, 2),
+            (yt, length, ext, 1),
+            (yti, length, length, 1),
+        ):
+            for half_index in range(2):
+                into.append(
+                    [tables_v[at + i * size : at + (i + 1) * size, :width] for i in range(parts)]
+                )
+                at += parts * size
+        backs = []
+        energy = jnp.zeros((SUB, length), jnp.float32)
+        for k in (0, 1):
+            left = jnp.concatenate(
+                [
+                    jnp.concatenate([main[2 * jp + k], shared[jp]], 1)
+                    for jp in range(plan.j // 2)
+                ],
+                0,
+            )
+            rows_z = mm3(halves(left), (zt[0][k], zt[1][k]))
+            rows_y = []
+            for jp in range(plan.j // 2):
+                full = mm3((yt[0][0], yt[1][0]), halves(rows_z[jp * ext : (jp + 1) * ext]))
+                squares = plane + square((2 * jp + k) * count + device)
+                weight = jnp.where(squares > 0.0, scale / jnp.maximum(squares, 1.0), 0.0)
+                weighted = full * weight
+                product = full * weighted
+                for i in range(length // SUB):
+                    energy += product[i * SUB : (i + 1) * SUB]
+                rows_y.append(mm3((yti[0][0], yti[1][0]), halves(weighted)))
+            backs.append(mm3(halves(jnp.concatenate(rows_y, 0)), (zti[0][k], zti[1][k])))
         for jp in range(plan.j // 2):
-            shared_back = None
+            here = slice(jp * length, (jp + 1) * length)
             for k in (0, 1):
-                j = 2 * jp + k
-                left = halves(jnp.concatenate([main[j], shared[jp]], 1))
-                rows_z = halves(mm3(left, (zt[0, k], zt[1, k])))
-                full = mm3((yt[0], yt[1]), rows_z)
-                p = j * count + device
-                wave_x = jnp.where(p <= length // 2, p, p - length // 2).astype(jnp.float32)
-                squares = wave_y + (wave_z + wave_x * wave_x)
-                weight = jnp.where(squares > 0.0, scale / jnp.maximum(squares, 1.0), 0.0)
-                weighted = halves(full * weight)
-                rows_y = halves(mm3((yti[0], yti[1]), weighted))
-                back = mm3(rows_y, (zti[0, k], zti[1, k]))
-                main[j, SUB : SUB + length, :] = back[:, :LANES]
-                part = back[:, LANES:]
-                shared_back = part if shared_back is None else shared_back + part
-            shared[jp, SUB : SUB + length, :] = shared_back
-        stride_back = plan.ny * per_back
+                main[2 * jp + k, SUB : SUB + length, :] = backs[k][here, :LANES]
+            shared[jp, SUB : SUB + length, :] = backs[0][here, LANES:] + backs[1][here, LANES:]
 
         def scatter(step, carry):
             jp = step // plan.ny
@@ -621,39 +775,69 @@
                 )
                 for k in (0, 1):
                     for zo, tile in enumerate((tiles[k][0], tiles[k][1], both[k])):
-                        start = b * per_back + (yo * plan.zo + zo) * plan.j + 2 * jp + k
-                        send[pl.ds(start, SUB, stride=stride_back), :] = tile
+                        ready[b, slot(yo * plan.zo + zo, jp, k)] = tile
             return carry
 
         lax.fori_loop(0, plan.ny * (plan.j // 2), scatter, 0)
 
-    smem = pl.BlockSpec(memory_space=pltpu.SMEM)
+        share = jnp.sum(energy) * (1.0 / count)
+
+        def pack(b, carry):
+            for row in TAIL[:2]:
+                ready[b, row] = jnp.full((SUB, LANES), share, jnp.float32)
+            for t in range(per_back // SUB):
+                tiles = turn_tiles([ready[b, t * SUB + i] for i in range(SUB)])
+                for a, tile in enumerate(tiles):
+                    send[a, b, t * SUB : (t + 1) * SUB, :] = tile
+            outgoing(b).start()
+            return carry
+
+        lax.fori_loop(0, plan.ny, pack, 0)
+        for b in range(plan.ny):
+            outgoing(b).wait()
+
+    hbm = pl.BlockSpec(memory_space=pltpu.HBM)
     vmem = pl.BlockSpec(memory_space=pltpu.VMEM)
     return pl.pallas_call(
         kernel,
         name="solve",
-        in_specs=[smem] + [vmem] * 8,
-        out_specs=vmem,
-        out_shape=jax.ShapeDtypeStruct((count * per_back, LANES), jnp.float32),
+        in_specs=[hbm, hbm, hbm],
+        out_specs=hbm,
+        out_shape=jax.ShapeDtypeStruct((plan.nz, plan.ny, per_back, LANES), jnp.float32),
+        compiler_params=pltpu.CompilerParams(vmem_limit_bytes=VMEM_LIMIT),
         scratch_shapes=[
+            pltpu.SMEM(t["window"].shape[1:], jnp.float32),
+            pltpu.VMEM((plan.nz, plan.ny, per, LANES), jnp.float32),
+            room(t["b"]),
+            pltpu.VMEM((plan.nz, plan.ny, per_back, LANES), jnp.float32),
             pltpu.VMEM((plan.j, ext, LANES), jnp.float32),
             pltpu.VMEM((plan.j // 2, ext, LANES), jnp.float32),
+            pltpu.VMEM((plan.ny, per, SUB, LANES), jnp.float32),
+            pltpu.VMEM((plan.ny, per_back, SUB, LANES), jnp.float32),
             pltpu.VMEM((count, LANES), jnp.float32),
             pltpu.SMEM((count, LANES), jnp.float32),
             pltpu.SemaphoreType.DMA,
+            pltpu.SemaphoreType.DMA((2,)),
+            pltpu.SemaphoreType.DMA((plan.ny,)),
+            pltpu.SemaphoreType.DMA((plan.ny,)),
         ],
         cost_estimate=pl.CostEstimate(flops=2_000_000_000, bytes_accessed=4_000_000, transcendentals=0),
     )
 
 
-def part_r(plan):
+def part_r(plan, t):
     length, fz, fy, count = plan.length, plan.fz, plan.fy, plan.count
     per = plan.rows_out
 
-    def kernel(recv, partial, fine, kron, out, field, lines, atoms_v, atoms, sem):
+    def kernel(
+        recv, partial_h, table_h, out_h,
+        partial, tables_v, out, field, lines, atoms_v, atoms, sem, sems,
+    ):
+        copies = fetch([(partial_h, partial), (table_h, tables_v)], sems)
         a = lax.axis_index("gz")
         b = lax.axis_index("gy")
-        atoms_v[...] = recv[pl.ds(plan.tail, count, stride=per), :]
+        for i in range(count):
+            atoms_v[i : i + 1, :] = recv[i, TAIL[0] : TAIL[0] + 1, :]
         copy = pltpu.make_async_copy(atoms_v, atoms, sem)
         copy.start()
         ahead = lax.rem(b + 1, plan.ny)
@@ -661,12 +845,16 @@
         lines[...] = jnp.zeros_like(lines)
         for source in range(plan.nz):
             for zz in range(2):
-                for slot, (origin, index) in enumerate(((behind, 0), (ahead, 0), (ahead, 2))):
-                    at = (source * plan.ny + origin) * per + plan.tail + index + zz
-                    lines[pl.ds(slot * GROUP + 2 * source + zz, 1), :] = recv[pl.ds(at, 1), :]
+                for number, (origin, index) in enumerate(((behind, 0), (ahead, 0), (ahead, 2))):
+                    at = TAIL[index + zz]
+                    into = number * GROUP + 2 * source + zz
+                    lines[into : into + 1, :] = recv[source * plan.ny + origin, at : at + 1, :]
         block = lines[...][:, LANES - plan.coarse :]
-        wide = sum(mm(piece, fine[...], NN) for piece in thirds(block)[::-1])
-        tall = sum(mm(kron[...], piece, NN) for piece in thirds(wide)[::-1])
+        for item in copies:
+            item.wait()
+        kron, fine = near_tables(plan, tables_v, 2 * count * SUB)
+        wide = sum(mm(piece, fine, NN) for piece in thirds(block)[::-1])
+        tall = sum(mm(kron, piece, NN) for piece in thirds(wide)[::-1])
         below, above, above2 = (tall[i * fz : (i + 1) * fz] for i in range(3))
         field[...] = jnp.zeros_like(field)
         field[1] = below * (-1.0 / 16.0)
@@ -708,136 +896,140 @@
         for i in range(fy // 2):
             span = slice(2 * i * length, (2 * i + 2) * length)
             out[:, span] = partial[:, span] + jnp.concatenate([field[2 * i], field[2 * i + 1]], 1)
-
+        for item in fetch([(out, out_h)], sems, 3):
+            item.wait()
+
+    hbm = pl.BlockSpec(memory_space=pltpu.HBM)
     vmem = pl.BlockSpec(memory_space=pltpu.VMEM)
     return pl.pallas_call(
         kernel,
         name="finish",
-        in_specs=[vmem] * 4,
-        out_specs=vmem,
+        compiler_params=pltpu.CompilerParams(vmem_limit_bytes=VMEM_LIMIT),
+        in_specs=[vmem, hbm, hbm],
+        out_specs=hbm,
         out_shape=jax.ShapeDtypeStruct((fz, fy * length), jnp.float32),
         scratch_shapes=[
+            pltpu.VMEM((fz, fy * length), jnp.float32),
+            room(t["a"]),
+            pltpu.VMEM((fz, fy * length), jnp.float32),
             pltpu.VMEM((fy, fz, length), jnp.float32),
             pltpu.VMEM((SUB * GROUP, LANES), jnp.float32),
             pltpu.VMEM((count, LANES), jnp.float32),
             pltpu.SMEM((count, LANES), jnp.float32),
             pltpu.SemaphoreType.DMA,
+            pltpu.SemaphoreType.DMA((4,)),
         ],
         cost_estimate=pl.CostEstimate(flops=3_000_000_000, bytes_accessed=4_000_000, transcendentals=0),
     )
 
 
-def part_c(plan, terms):
+def part_c(plan, t, terms):
     length, fz, fy, count = plan.length, plan.fz, plan.fy, plan.count
     per = plan.rows_back
-    span = GROUP * length
-
-    def kernel(recv, xt, history, residual, potential, sums, acc):
-        step = pl.program_id(0)
-        pieces = []
-        for zo in range(plan.zo):
-            spectrum = jnp.concatenate(
-                [
-                    recv[pl.ds((step * plan.zo + zo) * plan.j + j, count, stride=per), :]
-                    for j in range(plan.j)
-                ],
-                0,
+    wide = 3 * LANES
+
+    def kernel(
+        recv, table_h, history_h, potential_h, sums, tables_v, history, potential, sems
+    ):
+        first = fetch([(table_h, tables_v)], sems)
+        copies = fetch([(history_h.at[i], history.at[i]) for i in range(terms)], sems, 2)
+        first[0].wait()
+        size = count * SUB
+        xb = [
+            [tables_v[(4 * h + i) * size : (4 * h + i + 1) * size, :] for i in range(4)]
+            for h in range(2)
+        ]
+        def modes(t):
+            return halves(recv[:, t * SUB : (t + 1) * SUB, :].reshape(count * SUB, LANES).T)
+
+        def place(block, values):
+            yo, zo = block // plan.zo, block % plan.zo
+            for pair in range(GROUP // 2):
+                at = (yo * GROUP + 2 * pair) * length
+                rows = values[2 * pair * SUB : (2 * pair + 2) * SUB]
+                potential[zo * SUB : (zo + 1) * SUB, at : at + 2 * length] = jnp.concatenate(
+                    [rows[:SUB], rows[SUB:]], 1
+                )
+
+        given = [None, None]
+        for t in range(per // SUB):
+            left = modes(t)
+            place(t, mm3(left, (xb[0][0], xb[1][0])))
+            if t < 6:
+                part = mm3(left, (xb[0][1 + t % 3], xb[1][1 + t % 3]))
+                given[t // 3] = part if given[t // 3] is None else given[t // 3] + part
+        place(7, given[0])
+        place(8, given[1])
+        out = fetch([(potential, potential_h)], sems, 2 + terms)
+        acc = []
+        for i in range(terms):
+            def add(c, total, i=i):
+                cut = pl.ds(pl.multiple_of(c * wide, LANES), wide)
+                return total + history[i, :, cut] * potential[:, cut]
+
+            copies[i].wait()
+            acc.append(
+                lax.fori_loop(
+                    0, fy * length // wide, add, jnp.zeros((fz, wide), jnp.float32), unroll=4
+                )
             )
-            pieces.append(spectrum.T)
-        values = mm3(halves(jnp.concatenate(pieces, 0)), (xt[0], xt[1]))
-        for pair in range(GROUP // 2):
-            for zo in range(plan.zo):
-                at = zo * LANES + 2 * pair * SUB
-                potential[zo * SUB : (zo + 1) * SUB, 2 * pair * length : (2 * pair + 2) * length] = (
-                    jnp.concatenate([values[at : at + SUB], values[at + SUB : at + 2 * SUB]], 1)
-                )
-
-        @pl.when(step == 0)
-        def _():
-            acc[...] = jnp.zeros_like(acc)
-
-        wide = 3 * LANES
-        for i in range(terms + 1):
-            total = jnp.zeros((fz, wide), jnp.float32)
-            for c in range(span // wide):
-                cut = slice(c * wide, (c + 1) * wide)
-                other = history[i, :, cut] if i < terms else residual[:, cut]
-                total += other * potential[:, cut]
-            acc[i * SUB : (i + 1) * SUB, :] += sum(
-                total[r * SUB : (r + 1) * SUB, q * LANES : (q + 1) * LANES]
-                for r in range(plan.zo)
-                for q in range(3)
-            )
-
-        @pl.when(step == pl.num_programs(0) - 1)
-        def _():
-            lane = lax.broadcasted_iota(jnp.int32, (1, LANES), 1)
-            line = jnp.zeros((1, LANES), jnp.float32)
-            for i in range(terms + 1):
-                line = jnp.where(lane == i, jnp.sum(acc[i * SUB : (i + 1) * SUB, :]), line)
-            sums[...] = jnp.broadcast_to(line * (1.0 / float(length) ** 3), (count, LANES))
-
+        lane = lax.broadcasted_iota(jnp.int32, (1, LANES), 1)
+        line = jnp.zeros((1, LANES), jnp.float32)
+        for i in range(terms):
+            line = jnp.where(lane == i, jnp.sum(acc[i]), line)
+        own = jnp.sum(recv[:, TAIL[0] : TAIL[0] + 1, :], axis=0)
+        line = jnp.where(lane == terms, own, line)
+        sums[...] = jnp.broadcast_to(line * (1.0 / float(length) ** 3), (count, LANES))
+        out[0].wait()
+
+    hbm = pl.BlockSpec(memory_space=pltpu.HBM)
+    vmem = pl.BlockSpec(memory_space=pltpu.VMEM)
     return pl.pallas_call(
         kernel,
         name="finish_potential",
-        grid=(plan.yo,),
-        in_specs=[
-            pl.BlockSpec((count * per, LANES), lambda s: (0, 0)),
-            pl.BlockSpec((2, length, length), lambda s: (0, 0, 0)),
-            pl.BlockSpec((terms, fz, span), lambda s: (0, 0, s)),
-            pl.BlockSpec((fz, span), lambda s: (0, s)),
-        ],
-        out_specs=[
-            pl.BlockSpec((fz, span), lambda s: (0, s)),
-            pl.BlockSpec((count, LANES), lambda s: (0, 0)),
+        in_specs=[vmem, hbm, hbm],
+        out_specs=[hbm, vmem],
+        scratch_shapes=[
+            room(t["c"]),
+            pltpu.VMEM((terms, fz, fy * length), jnp.float32),
+            pltpu.VMEM((fz, fy * length), jnp.float32),
+            pltpu.SemaphoreType.DMA((3 + terms,)),
         ],
         out_shape=[
             jax.ShapeDtypeStruct((fz, fy * length), jnp.float32),
             jax.ShapeDtypeStruct((count, LANES), jnp.float32),
         ],
-        scratch_shapes=[pltpu.VMEM(((terms + 1) * SUB, LANES), jnp.float32)],
-        compiler_params=pltpu.CompilerParams(dimension_semantics=("arbitrary",)),
+        compiler_params=pltpu.CompilerParams(vmem_limit_bytes=LATE_LIMIT),
         cost_estimate=pl.CostEstimate(flops=500_000_000, bytes_accessed=10_000_000, transcendentals=0),
     )
 
 
-def exchange(sent, count, axes):
-    blocks = sent.reshape(count, sent.shape[0] // count, LANES)
-    return lax.all_to_all(blocks, axes, 0, 0, tiled=True).reshape(sent.shape)
+def exchange(sent, axes):
+    return lax.all_to_all(sent, axes, 0, 0, tiled=True)
 
 
 def local_fast(plan, coarse_density, density_in, history, atom_cell, atom_offset, atom_charge, atom_width):
     axes = ("gz", "gy")
     count = plan.count
     tables_ = fast_tables(plan)
-    sent, partial = part_a(plan)(
-        atom_cell.reshape(1, 1),
-        atom_offset.reshape(3, 1),
-        atom_charge.reshape(1, 1),
-        atom_width.reshape(1, 1),
+    sent, partial = part_a(plan, tables_)(
+        atom_cell.reshape(1),
+        atom_offset.reshape(3),
+        atom_charge.reshape(1),
+        atom_width.reshape(1),
         coarse_density,
         density_in,
-        tables_["fine"],
-        tables_["kron"],
-        tables_["x"],
-    )
-    spectra = exchange(sent, count, axes)
-    device = lax.axis_index("gz") * plan.ny + lax.axis_index("gy")
-    window = lax.dynamic_slice_in_dim(tables_["window"], device, 1, 0)
-    solved = part_b(plan)(
-        window,
-        spectra,
-        tables_["z"],
-        tables_["zt"],
-        tables_["y"],
-        tables_["yt"],
-        tables_["lanes"],
-        tables_["wave"],
-        tables_["wave_c"],
-    )
-    back = exchange(solved, count, axes)
-    residual = part_r(plan)(spectra, partial, tables_["fine"], tables_["kron"])
-    potential, sums = part_c(plan, history.shape[0])(back, tables_["x"], history, residual)
+        tables_["a"],
+    )
+    spectra = exchange(sent, axes)
+    solved = part_b(plan, tables_)(
+        tables_["window"],
+        spectra.reshape((plan.nz, plan.ny) + spectra.shape[1:]),
+        tables_["b"],
+    )
+    back = exchange(solved.reshape((count,) + solved.shape[2:]), axes)
+    residual = part_r(plan, tables_)(spectra, partial, tables_["a"])
+    potential, sums = part_c(plan, tables_, history.shape[0])(back, tables_["c"], history)
     rows = lax.all_to_all(sums, axes, 0, 0, tiled=True)
     return residual, potential, jnp.sum(rows, 0)[: history.shape[0] + 1]
 

time: 105 us -> 97.4 us (0.928)
  blocking collectives: 11.7 us -> 59.2 us
  waiting for transfers between devices: 40.7 us -> 1.58 us
  starting transfers between devices: 11.9 us -> 4.51 us
  local copies, waits for them, and re-layouts: 5.08 us -> 0.01 us
  Pallas kernels: 32.1 us -> 28.5 us
    all_to_all x1 -> x2, blocking collectives: 11.7 us -> 59.2 us  [exchange(): return lax.all_to_all(sent, axes, 0, 0, tiled=True)]
    all_to_all x2 -> x1, waiting for transfers between devices: 40.7 us -> 1.58 us  [local_fast(): rows = lax.all_to_all(sums, axes, 0, 0, tiled=True)]
    all_to_all x2 -> x1, starting transfers between devices: 11.9 us -> 4.51 us  [local_fast(): rows = lax.all_to_all(sums, axes, 0, 0, tiled=True)]
    pallas_call x4, Pallas kernels: 32.1 us -> 28.5 us  [the longest x1 13.9 us: local_fast(): part_b(plan, tables_)]
    dynamic_slice x1 -> x0, local copies, waits for them, and re-layouts: 1.42 us -> none  [local_fast(): window = lax.dynamic_slice_in_dim(tables_['window'], device, 1, 0)]
    another operation x1 -> x0, local copies, waits for them, and re-layouts: 1.41 us -> none
    reshape x1 -> x0, local copies, waits for them, and re-layouts: 1.31 us -> none  [local_fast(): atom_offset.reshape(3, 1)]
  transfers between devices with their start and end apart: 2 -> 1, of which waited for: 2 -> 1; matrix products, arithmetic and copies ran while one was open for 1% -> 0% of each run, Pallas kernels for 5% -> 6%
where the time goes in v1:
time: 97.4 us; the launch traced here: 96.9 us
  blocking collectives  59.2 us (61%)
  Pallas kernels  28.5 us (29%)
  starting transfers between devices  4.51 us (5%)
  between operations  2.62 us (3%)
  waiting for transfers between devices  1.58 us (2%)
    all_to_all x2, blocking collectives, exchange(): return lax.all_to_all(sent, axes, 0, 0, tiled=True)  59.2 us
    pallas_call x1, Pallas kernels, local_fast(): part_b(plan, tables_)  13.9 us
    pallas_call x1, Pallas kernels, local_fast(): residual = part_r(plan, tables_)(spectra, partial, tables_['a'])  5.6 us
    pallas_call x1, Pallas kernels, local_fast(): part_a(plan, tables_)  4.67 us
    all_to_all x1, starting transfers between devices, local_fast(): rows = lax.all_to_all(sums, axes, 0, 0, tiled=True)  4.51 us
    pallas_call x1, Pallas kernels, local_fast(): part_c(plan, tables_, history.shape[0])(back, tables_['c'], history)  4.35 us
  transfers between devices with their start and end apart: 1, of which 1 were waited for; matrix products, arithmetic and copies ran while one was open for 0% of the time, Pallas kernels for 6%

profile of v1, /device:TPU:0, one launch (start us, length us, event | category | flops | bytes accessed | tf_op | source)
XLA Modules:
  0.0 96.9 jit_solution(2209146540827122885)
XLA Ops:
  2.6 4.7 %spread.1 = (f32[32,64,128]{2,1,0:T(8,128)}, f32[24,9216]{1,0:T(8,128)}) custom-call(s32[1]{0:T(128)} %bitcast.10.cell_h, f32[3]{0:T(128)} %bitcast.16, f32[1]{0:T(128)} %bitcast.11.charge_h, f32[1]{0:T(128)} %bitcast.12.width_h, f32[96,24,96]{2,1,0:T(8,128)} %coarse_h.1, f32[24,9216]{1,0:T(8,128)} %density_h.1, bf16[800,192]{1,0:T(8,128)(2,1)} %constant.10.clone.table_h), custom_call_target="tpu_custom_call" | custom-call | flops 500000000 | bytes 4000000 | tf_op jit(solution)/shard_map/spread/pallas_call | solution.py:1015
  7.2 32.4 %all_to_all.19.recv = f32[32,64,128]{2,1,0:T(8,128)} all-to-all(f32[32,64,128]{2,1,0:T(8,128)} %get-tuple-element.7), channel_id=1, replica_groups=mesh['gz'=8,'gy'=4] {'gz','gy'}, dimensions={0} | all-to-all | bytes 2097152 | tf_op jit(solution)/shard_map/all_to_all | solution.py:1008
  39.6 13.9 %solve.1 = f32[8,4,56,128]{3,2,1,0:T(8,128)} custom-call(f32[32,1,1664]{2,1,0:T(1,128)} %constant.13.clone.window_h, f32[8,4,64,128]{3,2,1,0:T(8,128)} %bitcast.13, bf16[2560,256]{1,0:T(8,128)(2,1)} %constant.11.clone.table_h), custom_call_target="tpu_custom_call" | custom-call | flops 2000000000 | bytes 4000000 | tf_op jit(solution)/shard_map/solve/pallas_call | solution.py:1025
  53.5 0.0 copy-start
  53.5 26.8 %all_to_all.20.recv = f32[32,56,128]{2,1,0:T(8,128)S(1)} all-to-all(f32[32,56,128]{2,1,0:T(8,128)} %bitcast.14), channel_id=1, replica_groups=mesh['gz'=8,'gy'=4] {'gz','gy'}, dimensions={0} | all-to-all | bytes 1835008 | tf_op jit(solution)/shard_map/all_to_all | solution.py:1008
  80.3 0.0 copy-done
  80.3 4.3 %finish_potential.1 = (f32[24,9216]{1,0:T(8,128)}, f32[32,128]{1,0:T(8,128)}) custom-call(f32[32,56,128]{2,1,0:T(8,128)S(1)} %all_to_all.20.recv, bf16[2048,192]{1,0:T(8,128)(2,1)S(1)} %copy-done, f32[8,24,9216]{2,1,0:T(8,128)} %history_h.1), custom_call_target="tpu_custom_call" | custom-call | flops 500000000 | bytes 10000000 | tf_op jit(solution)/shard_map/finish_potential/pallas_call | solution.py:1032
  84.7 4.5 %all-to-all-start.2 = ((f32[32,1,128]{2,1,0:T(1,128)}), f32[32,1,128]{2,1,0:T(1,128)S(1)}, u32[]{:S(2)}, u32[]{:S(2)}) async-start(f32[32,1,128]{2,1,0:T(1,128)} %bitcast.7), calls=%async_computation.2 | async-start | bytes 32768 | tf_op jit(solution)/shard_map/all_to_all | solution.py:1033
  89.2 5.6 %finish.1 = f32[24,9216]{1,0:T(8,128)} custom-call(f32[32,64,128]{2,1,0:T(8,128)} %all_to_all.19.recv, f32[24,9216]{1,0:T(8,128)} %get-tuple-element.8.partial_h, bf16[800,192]{1,0:T(8,128)(2,1)} %constant.10.clone.table_h), custom_call_target="tpu_custom_call" | custom-call | flops 3000000000 | bytes 4000000 | tf_op jit(solution)/shard_map/finish/pallas_call | solution.py:1031
  94.8 1.6 %all-to-all-done.2 = f32[32,1,128]{2,1,0:T(1,128)S(1)} async-done(((f32[32,1,128]{2,1,0:T(1,128)}), f32[32,1,128]{2,1,0:T(1,128)S(1)}, u32[]{:S(2)}, u32[]{:S(2)}) %all-to-all-start.2) | async-done | bytes 16416 | tf_op jit(solution)/shard_map/all_to_all | solution.py:1033
  96.4 0.6 reduce_sum.9
Async XLA Ops:
  53.5 26.8 %copy-start = (bf16[2048,192]{1,0:T(8,128)(2,1)S(1)}, bf16[2048,192]{1,0:T(8,128)(2,1)}, u32[]{:S(2)}) copy-start(bf16[2048,192]{1,0:T(8,128)(2,1)} %constant.12.clone.table_h) | copy-start | bytes 2359300
  84.7 11.7 %all-to-all-start.2 = ((f32[32,1,128]{2,1,0:T(1,128)}), f32[32,1,128]{2,1,0:T(1,128)S(1)}, u32[]{:S(2)}, u32[]{:S(2)}) async-start(f32[32,1,128]{2,1,0:T(1,128)} %bitcast.7), calls=%async_computation.2 | async-start | bytes 32768 | tf_op jit(solution)/shard_map/all_to_all | solution.py:1033

commit v2 on v1

--- a/solution.py
+++ b/solution.py
@@ -283,8 +283,9 @@
     return pltpu.VMEM(array.shape, array.dtype)
 
 
-TAIL = (54, 55, 62, 63)
-EDGE = 56
+SPARE = 54
+PIECE = 40
+FACTS = 3 * PIECE
 VMEM_LIMIT = 60 * 1024 * 1024
 LATE_LIMIT = 48 * 1024 * 1024
 
@@ -326,7 +327,7 @@
         self.length, self.coarse, self.fz, self.fy = length, coarse, fz, fy
         self.j = length // self.count
         self.zo, self.yo = fz // SUB, fy // GROUP
-        self.rows_out = 64
+        self.rows_out = 56
         self.rows_back = 56
         self.ext = length + 32
 
@@ -337,10 +338,6 @@
             and self.fy % GROUP == 0
             and self.length == self.coarse * 2
         )
-
-
-def ext_slot(edge, zo):
-    return ((15, 3, 1)[edge] + 5 * zo) % GROUP
 
 
 def fast_tables(plan):
@@ -372,7 +369,6 @@
         return tables_z
 
     z_tables = along_z(np.arange(GROUP))
-    z_back = along_z((-np.arange(GROUP)) % GROUP)
     y_of_row = (np.arange(plan.ext) - SUB) % length
     count = plan.count
     x_window = np.zeros((count, length + GROUP, SUB), np.float32)
@@ -406,12 +402,28 @@
         )
 
     z_all = np.stack(z_tables).reshape(-1, length)
-    zt_all = np.stack([t.T for t in z_back]).reshape(-1, 2 * LANES)
+    coarse_z = fine_of.astype(np.float64) @ rows.T
+    own = plan.coarse // nz
+    edge_z = np.zeros((3, LANES, length))
+    for a in range(nz):
+        for edge in range(3):
+            at = PIECE * (a % 3) + own * edge
+            edge_z[a // 3, at : at + own] = coarse_z[a * own : (a + 1) * own]
+    y_table = np.zeros((length, plan.ext + GROUP))
+    y_table[:, : plan.ext] = rows[:, y_of_row]
+    for b in range(plan.ny):
+        at, y = plan.ext + 4 * b, b * plan.fy
+        y_table[:, at] = (9.0 * rows[:, y - 1] - rows[:, y - 3]) / 16.0
+        y_table[:, at + 1] = -rows[:, y - 1] / 16.0
+        y_table[:, at + 2] = -rows[:, (y + plan.fy + 1) % length] / 16.0
     near = [np.kron(np.eye(SUB), local_z), fine_of]
     return {
         "a": pack(halves_of(flat(padded)) + [table.astype(jnp.bfloat16) for table in near]),
         "b": pack(
-            halves_of(z_all) + halves_of(zt_all) + halves_of(rows[:, y_of_row]) + halves_of(rows.T)
+            halves_of(z_all)
+            + halves_of(edge_z.reshape(-1, length))
+            + halves_of(y_table)
+            + halves_of(rows.T)
         ),
         "c": pack(halves_of(np.stack([flat(kept)] + [flat(donors[i]) for i in range(3)]).reshape(-1, length))),
         "window": jnp.asarray(x_window.reshape(count, 1, -1)),
@@ -430,27 +442,50 @@
     per = plan.rows_out
 
     def kernel(
-        cell_h, offset_h, charge_h, width_h, coarse_h, density_h, table_h, send_h, partial_h,
-        cell, offset, charge, width, coarse, density, tables_v, send, partial, planes, smooth, field, donor, sems,
+        cell_h, offset_h, charge_h, width_h, coarse_h, density_h, table_h, send_h, partial_h, after_h, before_h,
+        cell, offset, charge, width, density, tables_v, send, partial, planes, smooth, field, after, before, sems,
     ):
-        first = fetch([(coarse_h, coarse), (table_h, tables_v)], sems)
-        second = fetch([(density_h, density)], sems, 3)
+        a = lax.axis_index("gz")
+        b = lax.axis_index("gy")
+        own = plan.coarse // plan.nz
+        first = fetch(
+            [
+                (
+                    coarse_h.at[lax.rem(own * a + plan.coarse - 1 + i, plan.coarse)],
+                    planes.at[pl.ds(i * rows_c, rows_c), :],
+                )
+                for i in range(GROUP)
+            ]
+            + [(table_h, tables_v)],
+            sems,
+            10,
+        )
+        third = fy // plan.yo * length
+        cuts = [slice(yo * third, (yo + 1) * third) for yo in range(plan.yo)]
+        order = (2, 0, 1)
+        second = {
+            yo: fetch([(density_h.at[:, cuts[yo]], density.at[:, cuts[yo]])], sems, 30 + yo)[0]
+            for yo in order
+        }
         facts_in = fetch(
             [(cell_h, cell), (offset_h, offset), (charge_h, charge), (width_h, width)], sems, 4
         )
         for copy in first:
             copy.wait()
         kron, fine = near_tables(plan, tables_v, 2 * count * SUB)
-        a = lax.axis_index("gz")
-        b = lax.axis_index("gy")
-        own = plan.coarse // plan.nz
-        for t in range(GROUP):
-            planes[pl.ds(t * rows_c, rows_c), :] = coarse[lax.rem(own * a + plan.coarse - 1 + t, plan.coarse)]
+        after[...] = planes[pl.ds(rows_c - 1, GROUP, stride=rows_c), :]
+        for i in range(2):
+            before[i * GROUP : (i + 1) * GROUP, :] = planes[pl.ds(i, GROUP, stride=rows_c), :]
+        out_halo = fetch([(after, after_h), (before, before_h)], sems, 0)
         for part in range(rows_c // SUB):
             block = jnp.concatenate(
                 [planes[pl.ds(part * SUB + y, GROUP, stride=rows_c), :] for y in range(SUB)], 0
             )
             wide = sum(mm(piece, fine, NN) for piece in thirds(block)[::-1])
+            if part == 0:
+                edges = [wide[i * GROUP + 1 : i * GROUP + 1 + own] for i in (0, 1)]
+            if part == rows_c // SUB - 1:
+                edges.append(wide[(SUB - 1) * GROUP + 1 : (SUB - 1) * GROUP + 1 + own])
             tall = sum(mm(kron, piece, NN) for piece in thirds(wide)[::-1])
             for y in range(SUB):
                 smooth[part * SUB + y] = tall[y * fz : (y + 1) * fz]
@@ -458,21 +493,19 @@
         def row(i):
             return smooth[i] if 0 <= i < rows_c else jnp.zeros((fz, length), jnp.float32)
 
-        second[0].wait()
-        for i in range(rows_c):
-            odd_row = (9.0 * (row(i) + row(i + 1)) - row(i - 1) - row(i + 2)) * (1.0 / 16.0)
-            old = density[:, 2 * i * length : (2 * i + 2) * length]
-            even_out = smooth[i] - old[:, :length]
-            odd_out = odd_row - old[:, length:]
-            field[2 * i] = even_out
-            field[2 * i + 1] = odd_out
-            partial[:, 2 * i * length : (2 * i + 2) * length] = jnp.concatenate([even_out, odd_out], 1)
-        edges = (
-            row(rows_c - 1) * (-1.0 / 16.0),
-            row(0) * (-1.0 / 16.0),
-            (9.0 * row(0) - row(1)) * (1.0 / 16.0),
-        )
-        out_partial = fetch([(partial, partial_h)], sems, 9)
+        def rows_of(yo):
+            second[yo].wait()
+            for i in range(yo * rows_c // plan.yo, (yo + 1) * rows_c // plan.yo):
+                odd_row = (9.0 * (row(i) + row(i + 1)) - row(i - 1) - row(i + 2)) * (1.0 / 16.0)
+                span = slice(2 * i * length, (2 * i + 2) * length)
+                old = density[:, span]
+                even_out = smooth[i] - old[:, :length]
+                odd_out = odd_row - old[:, length:]
+                field[2 * i] = even_out
+                field[2 * i + 1] = odd_out
+                partial[:, span] = jnp.concatenate([even_out, odd_out], 1)
+            return fetch([(partial.at[:, cuts[yo]], partial_h.at[:, cuts[yo]])], sems, 33 + yo)
+
         table = (tables_v[: count * SUB, :], tables_v[count * SUB : 2 * count * SUB, :])
         sub_row = lax.broadcasted_iota(jnp.int32, (count, SUB, LANES), 1)
 
@@ -483,32 +516,6 @@
                 for g in range(out.shape[1] // LANES)
             ]
 
-        for yo in (2, 0, 1):
-            block = jnp.concatenate(
-                [
-                    field[yo * GROUP + (-g) % GROUP, zo * SUB : (zo + 1) * SUB, :]
-                    for zo in range(plan.zo)
-                    for g in range(GROUP)
-                ],
-                0,
-            )
-            found = modes(block)
-            if yo == 2:
-                send[:, 48:56, :] = found[0]
-                donor[0] = found[1]
-                donor[1] = found[2]
-            else:
-                for pair in range(3):
-                    other = donor[yo]
-                    if pair < 2:
-                        other = pltpu.roll(other, 6 - 2 * pair, 1)
-                    at = SUB * (3 * yo + pair)
-                    send[:, at : at + SUB, :] = jnp.where(sub_row < 6, found[pair], other)
-        slots = [jnp.zeros((SUB, length), jnp.float32)] * GROUP
-        for zo in range(plan.zo):
-            for edge in range(3):
-                slots[ext_slot(edge, zo)] = edges[edge][zo * SUB : (zo + 1) * SUB]
-        send[:, EDGE : EDGE + SUB, :] = modes(jnp.concatenate(slots, 0))[0]
         for copy in facts_in:
             copy.wait()
         number = cell[0]
@@ -523,25 +530,43 @@
             charge[0],
             width[0],
         )
-        lane = lax.broadcasted_iota(jnp.int32, (1, LANES), 1)
-        atom = jnp.zeros((1, LANES), jnp.float32)
+        lane = lax.broadcasted_iota(jnp.int32, (count, SUB, LANES), 2)
+        spare = jnp.zeros((count, SUB, LANES), jnp.float32)
         for i, fact in enumerate(facts):
-            atom = jnp.where(lane == i, fact, atom)
-        send[:, TAIL[0] : TAIL[0] + 1, :] = jnp.broadcast_to(atom[None], (count, 1, LANES))
-        pad = jnp.zeros((1, LANES - plan.coarse), jnp.float32)
-        ahead = lax.rem(b + 1, plan.ny)
-        behind = lax.rem(b + plan.ny - 1, plan.ny)
-        for dest in range(plan.nz):
-            for zz in range(2):
-                p = lax.rem(own * dest + plan.coarse - 1 + 2 * a + zz, plan.coarse)
-                for edge, target, slot in ((rows_c - 1, ahead, 0), (0, behind, 0), (1, behind, 2)):
-                    line = jnp.concatenate([pad, coarse[p, edge : edge + 1, :]], 1)
-                    index = slot + zz
-                    if index == 0:
-                        line = jnp.where(lane < SUB, atom, line)
-                    send[dest * plan.ny + target, TAIL[index] : TAIL[index] + 1, :] = line
-        out_send = fetch([(send, send_h)], sems, 10)
-        for copy in out_partial + out_send:
+            spare = jnp.where(lane == FACTS + i, fact, spare)
+        gap = jnp.zeros((PIECE - 3 * own, length), jnp.float32)
+        rest = jnp.zeros((LANES - FACTS, length), jnp.float32)
+        edge_modes = modes(jnp.concatenate((edges + [gap]) * 3 + [rest], 0))[0]
+        for j in range(plan.j):
+            into = 6 + j // 3
+            here = (lane // PIECE == j % 3) & (sub_row == into)
+            spare = jnp.where(here, pltpu.roll(edge_modes, (into - j) % SUB, 1), spare)
+        donor = None
+        outs = []
+        for yo in order:
+            outs += rows_of(yo)
+            block = jnp.concatenate(
+                [
+                    field[yo * GROUP + (-g) % GROUP, zo * SUB : (zo + 1) * SUB, :]
+                    for zo in range(plan.zo)
+                    for g in range(GROUP)
+                ],
+                0,
+            )
+            found = modes(block)
+            if yo == 2:
+                send[:, 48:56, :] = jnp.where(sub_row < 6, found[0], spare)
+                donor = found[1:]
+            else:
+                for pair in range(3):
+                    other = donor[yo]
+                    if pair < 2:
+                        other = pltpu.roll(other, 6 - 2 * pair, 1)
+                    at = SUB * (3 * yo + pair)
+                    send[:, at : at + SUB, :] = jnp.where(sub_row < 6, found[pair], other)
+            span = slice(48, 56) if yo == 2 else slice(24 * yo, 24 * yo + 24)
+            outs += fetch([(send.at[:, span, :], send_h.at[:, span, :])], sems, 27 + yo)
+        for copy in out_halo + outs:
             copy.wait()
 
     hbm = pl.BlockSpec(memory_space=pltpu.HBM)
@@ -549,10 +574,12 @@
         kernel,
         name="spread",
         in_specs=[hbm] * 7,
-        out_specs=[hbm, hbm],
+        out_specs=[hbm] * 4,
         out_shape=[
             jax.ShapeDtypeStruct((count, per, LANES), jnp.float32),
             jax.ShapeDtypeStruct((fz, fy * length), jnp.float32),
+            jax.ShapeDtypeStruct((GROUP, plan.coarse), jnp.float32),
+            jax.ShapeDtypeStruct((2 * GROUP, plan.coarse), jnp.float32),
         ],
         compiler_params=pltpu.CompilerParams(vmem_limit_bytes=VMEM_LIMIT),
         scratch_shapes=[
@@ -560,7 +587,6 @@
             pltpu.SMEM((3,), jnp.float32),
             pltpu.SMEM((1,), jnp.float32),
             pltpu.SMEM((1,), jnp.float32),
-            pltpu.VMEM((plan.coarse, rows_c, plan.coarse), jnp.float32),
             pltpu.VMEM((fz, fy * length), jnp.float32),
             room(t["a"]),
             pltpu.VMEM((count, per, LANES), jnp.float32),
@@ -568,8 +594,9 @@
             pltpu.VMEM((GROUP * rows_c, plan.coarse), jnp.float32),
             pltpu.VMEM((rows_c, fz, length), jnp.float32),
             pltpu.VMEM((fy, fz, length), jnp.float32),
-            pltpu.VMEM((2, count, SUB, LANES), jnp.float32),
-            pltpu.SemaphoreType.DMA((11,)),
+            pltpu.VMEM((GROUP, plan.coarse), jnp.float32),
+            pltpu.VMEM((2 * GROUP, plan.coarse), jnp.float32),
+            pltpu.SemaphoreType.DMA((36,)),
         ],
         cost_estimate=pl.CostEstimate(flops=500_000_000, bytes_accessed=4_000_000, transcendentals=0),
     )
@@ -587,7 +614,7 @@
 
     def kernel(
         window_h, recv_h, table_h, send_h,
-        window, recv, tables_v, send, main, shared, turned, ready, atoms_v, atoms, sem, sems, sems_in, sems_out,
+        window, recv, tables_v, send, main, shared, bells, turned, ready, atoms_v, atoms, sem, sems, sems_in, sems_out,
     ):
         device = lax.axis_index("gz") * plan.ny + lax.axis_index("gy")
 
@@ -614,42 +641,22 @@
                 )
                 for i, tile in enumerate(tiles):
                     turned[b, t * SUB + i] = tile
-            atoms_v[pl.ds(pl.multiple_of(b * SUB, SUB), SUB), :] = turned[b, TAIL[0]]
+            atoms_v[pl.ds(pl.multiple_of(b * SUB, SUB), SUB), :] = turned[b, SPARE]
             return carry
 
         lax.fori_loop(0, plan.ny, unpack, 0)
         copy = pltpu.make_async_copy(atoms_v, atoms, sem)
         copy.start()
         masks = tile_masks()
-        group = masks[1]
-        for j in range(plan.j):
-            main[j, :SUB, :] = jnp.zeros((SUB, LANES), jnp.float32)
-            main[j, SUB + length :, :] = jnp.zeros((ext - SUB - length, LANES), jnp.float32)
-        for jp in range(plan.j // 2):
-            shared[jp, :SUB, :] = jnp.zeros((SUB, LANES), jnp.float32)
-            shared[jp, SUB + length :, :] = jnp.zeros((ext - SUB - length, LANES), jnp.float32)
-        def gather(step, carry):
-            jp = step // plan.ny
-            b = lax.rem(step, plan.ny)
-            edge_ahead = lax.rem(b + 1, plan.ny)
-            edge_behind = lax.rem(b + plan.ny - 1, plan.ny)
-            edges = []
-            for source in (edge_behind, edge_ahead):
-                edges.append([turned[source, EDGE + 2 * jp + k] for k in (0, 1)])
+        bells[...] = jnp.zeros_like(bells)
+        def gather(jp, b):
             for yo in range(plan.yo):
                 tiles = []
                 for k in (0, 1):
                     for zo in range(plan.zo):
                         tile = turned[b, slot(yo * plan.zo + zo, jp, k)]
-                        shift = (LANES - 5 * zo * SUB) % LANES
-                        if yo == 0:
-                            extra = pltpu.roll(edges[0][k], shift, 1) if shift else edges[0][k]
-                            tile = jnp.where(group == 15, tile + extra, tile)
-                        if yo == plan.yo - 1:
-                            extra = pltpu.roll(edges[1][k], shift, 1) if shift else edges[1][k]
-                            tile = jnp.where((group == 3) | (group == 1), tile + extra, tile)
                         tiles.append(tile)
-                at = pl.multiple_of(SUB + b * plan.fy + yo * GROUP, SUB)
+                at = pl.multiple_of(b * plan.fy + yo * GROUP, SUB)
                 for k in (0, 1):
                     upper, lower = block_turn(tiles[3 * k], tiles[3 * k + 1], masks)
                     main[2 * jp + k, pl.ds(at, SUB), :] = upper
@@ -657,12 +664,13 @@
                 upper, lower = block_turn(tiles[2], tiles[5], masks)
                 shared[jp, pl.ds(at, SUB), :] = upper
                 shared[jp, pl.ds(at + SUB, SUB), :] = lower
+        def gather_alone(b, carry):
+            gather(0, b)
             return carry
 
-        lax.fori_loop(0, plan.ny * (plan.j // 2), gather, 0)
+        lax.fori_loop(0, plan.ny, gather_alone, 0)
         copy.wait()
-        for item in copies:
-            item.wait()
+        copies[0].wait()
         lane = lax.broadcasted_iota(jnp.int32, (1, LANES), 1)
         block = lane // SUB
         odd = block >= SUB
@@ -671,10 +679,8 @@
         z_shared = (z_first + 2 * SUB).astype(jnp.float32)
         window_rows = lax.broadcasted_iota(jnp.int32, (GROUP, LANES), 0).astype(jnp.float32) - RC
 
-        def deposit(i, carry):
-            z0, y0, x0 = atoms[i, 0], atoms[i, 1], atoms[i, 2]
-            off_z, off_y, off_x = atoms[i, 3], atoms[i, 4], atoms[i, 5]
-            charge, width = atoms[i, 6], atoms[i, 7]
+        def deposit(i):
+            z0, y0, x0, off_z, off_y, off_x, charge, width = (atoms[i, FACTS + f] for f in range(8))
             ratio = jnp.full((SUB, LANES), width / jnp.pi, jnp.float32)
             factor = ratio * jnp.sqrt(ratio) * charge
             factor = factor[0:1]
@@ -700,11 +706,20 @@
             at = y0.astype(jnp.int32) - RC + SUB
             for jp in range(plan.j // 2):
                 for k in (0, 1):
-                    main[2 * jp + k, pl.ds(at, GROUP), :] += sums[jp][k] * factor
-                shared[jp, pl.ds(at, GROUP), :] += sums[jp][2] * factor
+                    bells[2 * jp + k, pl.ds(at, GROUP), :] += sums[jp][k] * factor
+                bells[plan.j + jp, pl.ds(at, GROUP), :] += sums[jp][2] * factor
+
+        steps = plan.ny * (plan.j // 2 - 1)
+
+        def gather_and_deposit(step, carry):
+            for i in range(count // steps):
+                deposit(step * (count // steps) + i)
+            gather(1 + step // plan.ny, lax.rem(step, plan.ny))
             return carry
 
-        lax.fori_loop(0, count, deposit, 0)
+        lax.fori_loop(0, steps, gather_and_deposit, 0)
+        for item in copies[1:]:
+            item.wait()
         scale = float(length) ** 2 / math.pi
         half = length // 2
 
@@ -715,12 +730,12 @@
         plane = square(lax.broadcasted_iota(jnp.int32, (length, length), 0)) + square(
             lax.broadcasted_iota(jnp.int32, (length, length), 1)
         )
-        zt, zti, yt, yti = [], [], [], []
+        zt, et, yt, yti = [], [], [], []
         at = 0
         for into, size, width, parts in (
             (zt, 2 * LANES, length, 2),
-            (zti, length, 2 * LANES, 2),
-            (yt, length, ext, 1),
+            (et, 3 * LANES, length, 1),
+            (yt, length, ext + GROUP, 1),
             (yti, length, length, 1),
         ):
             for half_index in range(2):
@@ -728,12 +743,48 @@
                     [tables_v[at + i * size : at + (i + 1) * size, :width] for i in range(parts)]
                 )
                 at += parts * size
+        edge_row = lax.broadcasted_iota(jnp.int32, (GROUP, LANES), 0)
+        edge_lane = lax.broadcasted_iota(jnp.int32, (GROUP, LANES), 1)
+        own = plan.coarse // plan.nz
+        first_lane = own * (edge_row & 3)
+        lines = []
+        for row in range(2):
+            spread = [turned[b, SPARE + row] for b in range(plan.ny)]
+            for q in range(3):
+                blocks = []
+                for a in range(plan.nz):
+                    if a % 3 == 0:
+                        blocks.append(jnp.zeros((GROUP, LANES), jnp.float32))
+                    line = jnp.concatenate(
+                        [jnp.broadcast_to(tile[a : a + 1], (4, LANES)) for tile in spread], 0
+                    )
+                    shift = (PIECE * (a % 3 - q)) % LANES
+                    line = pltpu.roll(line, shift, 1) if shift else line
+                    start = first_lane + PIECE * (a % 3)
+                    keep = (edge_lane >= start) & (edge_lane < start + own) & ((edge_row & 3) < 3)
+                    blocks[-1] = jnp.where(keep, line, blocks[-1])
+                lines.append(jnp.concatenate(blocks, 1))
+        edges_z = mm3(halves(jnp.concatenate(lines, 0)), (et[0][0], et[1][0]))
+        def with_bells(block, index):
+            top, last = SUB, SUB + length
+            return jnp.concatenate(
+                [
+                    bells[index, :top, :],
+                    block + bells[index, top:last, :],
+                    bells[index, last:, :],
+                ],
+                0,
+            )
+
         backs = []
         energy = jnp.zeros((SUB, length), jnp.float32)
         for k in (0, 1):
             left = jnp.concatenate(
                 [
-                    jnp.concatenate([main[2 * jp + k], shared[jp]], 1)
+                    jnp.concatenate(
+                        [with_bells(main[2 * jp + k], 2 * jp + k), with_bells(shared[jp], plan.j + jp)],
+                        1,
+                    )
                     for jp in range(plan.j // 2)
                 ],
                 0,
@@ -741,7 +792,11 @@
             rows_z = mm3(halves(left), (zt[0][k], zt[1][k]))
             rows_y = []
             for jp in range(plan.j // 2):
-                full = mm3((yt[0][0], yt[1][0]), halves(rows_z[jp * ext : (jp + 1) * ext]))
+                j = 2 * jp + k
+                column = jnp.concatenate(
+                    [rows_z[jp * ext : (jp + 1) * ext], edges_z[j * GROUP : (j + 1) * GROUP]], 0
+                )
+                full = mm3((yt[0][0], yt[1][0]), halves(column))
                 squares = plane + square((2 * jp + k) * count + device)
                 weight = jnp.where(squares > 0.0, scale / jnp.maximum(squares, 1.0), 0.0)
                 weighted = full * weight
@@ -749,32 +804,30 @@
                 for i in range(length // SUB):
                     energy += product[i * SUB : (i + 1) * SUB]
                 rows_y.append(mm3((yti[0][0], yti[1][0]), halves(weighted)))
-            backs.append(mm3(halves(jnp.concatenate(rows_y, 0)), (zti[0][k], zti[1][k])))
+            backs.append(mm3(halves(jnp.concatenate(rows_y, 0)), (zt[0][k], zt[1][k]), NT))
         for jp in range(plan.j // 2):
             here = slice(jp * length, (jp + 1) * length)
             for k in (0, 1):
-                main[2 * jp + k, SUB : SUB + length, :] = backs[k][here, :LANES]
-            shared[jp, SUB : SUB + length, :] = backs[0][here, LANES:] + backs[1][here, LANES:]
+                main[2 * jp + k] = backs[k][here, :LANES]
+            shared[jp] = backs[0][here, LANES:] + backs[1][here, LANES:]
+
+        first = masks[0] == 0
 
         def scatter(step, carry):
             jp = step // plan.ny
             b = lax.rem(step, plan.ny)
             for yo in range(plan.yo):
-                at = pl.multiple_of(SUB + b * plan.fy + yo * GROUP, SUB)
-                tiles = []
+                at = pl.multiple_of(b * plan.fy + yo * GROUP, SUB)
+                found = []
+                for source in (main.at[2 * jp], main.at[2 * jp + 1], shared.at[jp]):
+                    upper, lower = block_turn(
+                        source[pl.ds(at, SUB), :], source[pl.ds(at + SUB, SUB), :], masks
+                    )
+                    found.append(
+                        (jnp.where(first, upper, lower), jnp.where(first, lower, upper))
+                    )
                 for k in (0, 1):
-                    tiles.append(
-                        block_turn(
-                            main[2 * jp + k, pl.ds(at, SUB), :],
-                            main[2 * jp + k, pl.ds(at + SUB, SUB), :],
-                            masks,
-                        )
-                    )
-                both = block_turn(
-                    shared[jp, pl.ds(at, SUB), :], shared[jp, pl.ds(at + SUB, SUB), :], masks
-                )
-                for k in (0, 1):
-                    for zo, tile in enumerate((tiles[k][0], tiles[k][1], both[k])):
+                    for zo, tile in enumerate((found[k][0], found[k][1], found[2][k])):
                         ready[b, slot(yo * plan.zo + zo, jp, k)] = tile
             return carry
 
@@ -783,11 +836,12 @@
         share = jnp.sum(energy) * (1.0 / count)
 
         def pack(b, carry):
-            for row in TAIL[:2]:
+            for row in (SPARE, SPARE + 1):
                 ready[b, row] = jnp.full((SUB, LANES), share, jnp.float32)
             for t in range(per_back // SUB):
                 tiles = turn_tiles([ready[b, t * SUB + i] for i in range(SUB)])
-                for a, tile in enumerate(tiles):
+                for i, tile in enumerate(tiles):
+                    a = (SUB - i) % SUB
                     send[a, b, t * SUB : (t + 1) * SUB, :] = tile
             outgoing(b).start()
             return carry
@@ -810,8 +864,9 @@
             pltpu.VMEM((plan.nz, plan.ny, per, LANES), jnp.float32),
             room(t["b"]),
             pltpu.VMEM((plan.nz, plan.ny, per_back, LANES), jnp.float32),
-            pltpu.VMEM((plan.j, ext, LANES), jnp.float32),
-            pltpu.VMEM((plan.j // 2, ext, LANES), jnp.float32),
+            pltpu.VMEM((plan.j, length, LANES), jnp.float32),
+            pltpu.VMEM((plan.j // 2, length, LANES), jnp.float32),
+            pltpu.VMEM((plan.j + plan.j // 2, ext, LANES), jnp.float32),
             pltpu.VMEM((plan.ny, per, SUB, LANES), jnp.float32),
             pltpu.VMEM((plan.ny, per_back, SUB, LANES), jnp.float32),
             pltpu.VMEM((count, LANES), jnp.float32),
@@ -830,29 +885,29 @@
     per = plan.rows_out
 
     def kernel(
-        recv, partial_h, table_h, out_h,
+        recv, partial_h, below_h, above_h, table_h, out_h,
         partial, tables_v, out, field, lines, atoms_v, atoms, sem, sems,
     ):
-        copies = fetch([(partial_h, partial), (table_h, tables_v)], sems)
+        lines[...] = jnp.zeros_like(lines)
+        copies = fetch(
+            [
+                (partial_h, partial),
+                (table_h, tables_v),
+                (below_h, lines.at[pl.ds(0, GROUP), :]),
+                (above_h, lines.at[pl.ds(GROUP, 2 * GROUP), :]),
+            ],
+            sems,
+        )
         a = lax.axis_index("gz")
         b = lax.axis_index("gy")
         for i in range(count):
-            atoms_v[i : i + 1, :] = recv[i, TAIL[0] : TAIL[0] + 1, :]
+            atoms_v[i : i + 1, :] = recv[i, SPARE : SPARE + 1, :]
         copy = pltpu.make_async_copy(atoms_v, atoms, sem)
         copy.start()
-        ahead = lax.rem(b + 1, plan.ny)
-        behind = lax.rem(b + plan.ny - 1, plan.ny)
-        lines[...] = jnp.zeros_like(lines)
-        for source in range(plan.nz):
-            for zz in range(2):
-                for number, (origin, index) in enumerate(((behind, 0), (ahead, 0), (ahead, 2))):
-                    at = TAIL[index + zz]
-                    into = number * GROUP + 2 * source + zz
-                    lines[into : into + 1, :] = recv[source * plan.ny + origin, at : at + 1, :]
-        block = lines[...][:, LANES - plan.coarse :]
         for item in copies:
             item.wait()
         kron, fine = near_tables(plan, tables_v, 2 * count * SUB)
+        block = lines[...]
         wide = sum(mm(piece, fine, NN) for piece in thirds(block)[::-1])
         tall = sum(mm(kron, piece, NN) for piece in thirds(wide)[::-1])
         below, above, above2 = (tall[i * fz : (i + 1) * fz] for i in range(3))
@@ -865,21 +920,21 @@
         x_here = lax.broadcasted_iota(jnp.int32, (fz, length), 1).astype(jnp.float32)
 
         def deposit(i, carry):
-            z0 = wrapped(atoms[i, 0] - (a * fz).astype(jnp.float32), length)
-            y0 = wrapped(atoms[i, 1] - (b * fy).astype(jnp.float32), length).astype(jnp.int32)
+            z0 = wrapped(atoms[i, FACTS + 0] - (a * fz).astype(jnp.float32), length)
+            y0 = wrapped(atoms[i, FACTS + 1] - (b * fy).astype(jnp.float32), length).astype(jnp.int32)
             first = jnp.maximum(y0 - RC, 0)
             last = jnp.minimum(y0 + RC + 2, fy)
             near_z = (z0 > -RC - 2.0) & (z0 < fz + RC + 1.0)
 
             @pl.when(near_z & (first < last))
             def _():
-                off_z, off_y, off_x = atoms[i, 3], atoms[i, 4], atoms[i, 5]
-                charge, width = atoms[i, 6], atoms[i, 7]
+                off_z, off_y, off_x = atoms[i, FACTS + 3], atoms[i, FACTS + 4], atoms[i, FACTS + 5]
+                charge, width = atoms[i, FACTS + 6], atoms[i, FACTS + 7]
                 ratio = jnp.full((fz, length), width / jnp.pi, jnp.float32)
                 factor = ratio * jnp.sqrt(ratio) * charge
                 cut = jnp.exp(jnp.full((fz, length), -width * float(RC * RC), jnp.float32))
                 dist_z = z_here - z0 - off_z
-                dist_x = wrapped(x_here - atoms[i, 2], length) - off_x
+                dist_x = wrapped(x_here - atoms[i, FACTS + 2], length) - off_x
                 flat = dist_z * dist_z + dist_x * dist_x
 
                 def row(y, inner):
@@ -896,7 +951,7 @@
         for i in range(fy // 2):
             span = slice(2 * i * length, (2 * i + 2) * length)
             out[:, span] = partial[:, span] + jnp.concatenate([field[2 * i], field[2 * i + 1]], 1)
-        for item in fetch([(out, out_h)], sems, 3):
+        for item in fetch([(out, out_h)], sems, 4):
             item.wait()
 
     hbm = pl.BlockSpec(memory_space=pltpu.HBM)
@@ -905,7 +960,7 @@
         kernel,
         name="finish",
         compiler_params=pltpu.CompilerParams(vmem_limit_bytes=VMEM_LIMIT),
-        in_specs=[vmem, hbm, hbm],
+        in_specs=[vmem] + [hbm] * 4,
         out_specs=hbm,
         out_shape=jax.ShapeDtypeStruct((fz, fy * length), jnp.float32),
         scratch_shapes=[
@@ -913,11 +968,11 @@
             room(t["a"]),
             pltpu.VMEM((fz, fy * length), jnp.float32),
             pltpu.VMEM((fy, fz, length), jnp.float32),
-            pltpu.VMEM((SUB * GROUP, LANES), jnp.float32),
+            pltpu.VMEM((SUB * GROUP, plan.coarse), jnp.float32),
             pltpu.VMEM((count, LANES), jnp.float32),
             pltpu.SMEM((count, LANES), jnp.float32),
             pltpu.SemaphoreType.DMA,
-            pltpu.SemaphoreType.DMA((4,)),
+            pltpu.SemaphoreType.DMA((5,)),
         ],
         cost_estimate=pl.CostEstimate(flops=3_000_000_000, bytes_accessed=4_000_000, transcendentals=0),
     )
@@ -977,7 +1032,7 @@
         line = jnp.zeros((1, LANES), jnp.float32)
         for i in range(terms):
             line = jnp.where(lane == i, jnp.sum(acc[i]), line)
-        own = jnp.sum(recv[:, TAIL[0] : TAIL[0] + 1, :], axis=0)
+        own = jnp.sum(recv[:, SPARE : SPARE + 1, :], axis=0)
         line = jnp.where(lane == terms, own, line)
         sums[...] = jnp.broadcast_to(line * (1.0 / float(length) ** 3), (count, LANES))
         out[0].wait()
@@ -1012,7 +1067,7 @@
     axes = ("gz", "gy")
     count = plan.count
     tables_ = fast_tables(plan)
-    sent, partial = part_a(plan, tables_)(
+    sent, partial, after, before = part_a(plan, tables_)(
         atom_cell.reshape(1),
         atom_offset.reshape(3),
         atom_charge.reshape(1),
@@ -1028,7 +1083,10 @@
         tables_["b"],
     )
     back = exchange(solved.reshape((count,) + solved.shape[2:]), axes)
-    residual = part_r(plan, tables_)(spectra, partial, tables_["a"])
+    ring = [(i, (i + 1) % plan.ny) for i in range(plan.ny)]
+    below = lax.ppermute(after, "gy", ring)
+    above = lax.ppermute(before, "gy", [(target, source) for source, target in ring])
+    residual = part_r(plan, tables_)(spectra, partial, below, above, tables_["a"])
     potential, sums = part_c(plan, tables_, history.shape[0])(back, tables_["c"], history)
     rows = lax.all_to_all(sums, axes, 0, 0, tiled=True)
     return residual, potential, jnp.sum(rows, 0)[: history.shape[0] + 1]

time: 97.4 us -> 94.3 us (0.968)
  blocking collectives: 59.2 us -> 29.7 us
  waiting for transfers between devices: 1.58 us -> 19.5 us
  starting transfers between devices: 4.51 us -> 13.2 us
    all_to_all x2 -> x1, blocking collectives: 59.2 us -> 29.7 us  [exchange(): return lax.all_to_all(sent, axes, 0, 0, tiled=True)]
    all_to_all x0 -> x1, waiting for transfers between devices: none -> 18.5 us  [exchange(): return lax.all_to_all(sent, axes, 0, 0, tiled=True)]
    all_to_all x0 -> x1, starting transfers between devices: none -> 4.51 us  [exchange(): return lax.all_to_all(sent, axes, 0, 0, tiled=True)]
    ppermute x0 -> x2, starting transfers between devices: none -> 3.88 us  [the longest x1 2.05 us: local_fast(): lax.ppermute(before, 'gy', [(target, source) for source, target in ring])]
    pallas_call x1, Pallas kernels: 13.9 us -> 12.8 us  [local_fast(): part_b(plan, tables_)]
  transfers between devices with their start and end apart: 1 -> 4, of which waited for: 1 -> 2; matrix products, arithmetic and copies ran while one was open for 0% -> 0% of each run, Pallas kernels for 6% -> 10%
where the time goes in v2:
time: 94.3 us; the launch traced here: 93.9 us
  blocking collectives  29.7 us (31%)
  Pallas kernels  27.7 us (29%)
  waiting for transfers between devices  19.5 us (21%)
  starting transfers between devices  13.2 us (14%)
  between operations  2.68 us (3%)
    all_to_all x1, blocking collectives, exchange(): return lax.all_to_all(sent, axes, 0, 0, tiled=True)  29.7 us
    all_to_all x1, waiting for transfers between devices, exchange(): return lax.all_to_all(sent, axes, 0, 0, tiled=True)  18.5 us
    pallas_call x1, Pallas kernels, local_fast(): part_b(plan, tables_)  12.8 us
    pallas_call x1, Pallas kernels, local_fast(): part_r(plan, tables_)(spectra, partial, below, above, tables_['a'])  5.49 us
    pallas_call x1, Pallas kernels, local_fast(): part_a(plan, tables_)  5.05 us
    all_to_all x1, starting transfers between devices, local_fast(): rows = lax.all_to_all(sums, axes, 0, 0, tiled=True)  4.78 us
    all_to_all x1, starting transfers between devices, exchange(): return lax.all_to_all(sent, axes, 0, 0, tiled=True)  4.51 us
    pallas_call x1, Pallas kernels, local_fast(): part_c(plan, tables_, history.shape[0])(back, tables_['c'], history)  4.35 us
  transfers between devices with their start and end apart: 4, of which 2 were waited for; matrix products, arithmetic and copies ran while one was open for 0% of the time, Pallas kernels for 10%

profile of v2, /device:TPU:0, one launch (start us, length us, event | category | flops | bytes accessed | tf_op | source)
XLA Modules:
  0.0 93.9 jit_solution(13666406442294141747)
XLA Ops:
  2.6 5.0 %spread.1 = (f32[32,56,128]{2,1,0:T(8,128)}, f32[24,9216]{1,0:T(8,128)}, f32[16,96]{1,0:T(8,128)}, f32[32,96]{1,0:T(8,128)}) custom-call(s32[1]{0:T(128)} %bitcast.10.cell_h, f32[3]{0:T(128)} %bitcast.16, f32[1]{0:T(128)} %bitcast.11.charge_h, f32[1]{0:T(128)} %bitcast.12.width_h, f32[96,24,96]{2,1,0:T(8,128)} %coarse_h.1, f32[24,9216]{1,0:T(8,128)} %density_h.1, ...), custom_call_target="tpu_custom_call" | custom-call | flops 500000000 | bytes 4000000 | tf_op jit(solution)/shard_map/spread/pallas_call | solution.py:1070
  7.6 29.7 %all_to_all.19.recv = f32[32,56,128]{2,1,0:T(8,128)} all-to-all(f32[32,56,128]{2,1,0:T(8,128)} %get-tuple-element.9), channel_id=1, replica_groups=mesh['gz'=8,'gy'=4] {'gz','gy'}, dimensions={0} | all-to-all | bytes 1835008 | tf_op jit(solution)/shard_map/all_to_all | solution.py:1063
  37.3 12.8 %solve.1 = f32[8,4,56,128]{3,2,1,0:T(8,128)} custom-call(f32[32,1,1664]{2,1,0:T(1,128)} %constant.13.clone.window_h, f32[8,4,56,128]{3,2,1,0:T(8,128)} %bitcast.13, bf16[2560,240]{1,0:T(8,128)(2,1)} %constant.11.clone.table_h), custom_call_target="tpu_custom_call" | custom-call | flops 2000000000 | bytes 4000000 | tf_op jit(solution)/shard_map/solve/pallas_call | solution.py:1080
  50.1 0.0 copy-start.3
  50.1 0.0 copy-start.1
  50.1 0.0 copy-start
  50.1 4.5 %all-to-all-start.1 = ((f32[32,56,128]{2,1,0:T(8,128)}), f32[32,56,128]{2,1,0:T(8,128)S(1)}, u32[]{:S(2)}, u32[]{:S(2)}) async-start(f32[32,56,128]{2,1,0:T(8,128)} %bitcast.14), calls=%async_computation.1 | async-start | bytes 1835008 | tf_op jit(solution)/shard_map/all_to_all | solution.py:1063
  54.6 0.0 copy-done.3
  54.6 1.8 %collective-permute-start = (f32[16,96]{1,0:T(8,128)S(1)}, f32[16,96]{1,0:T(8,128)S(1)}, u32[]{:S(2)}, u32[]{:S(2)}) collective-permute-start(f32[16,96]{1,0:T(8,128)S(1)} %copy-done.3), channel_id=1, source_target_pairs={{0,1},{1,2},{2,3},{3,0},{4,5},{5,6},{6,7},{7,4},{8,9},{9,10},{10,1... | collective-permute-start | bytes 18440 | tf_op jit(solution)/shard_map/ppermute | solution.py:1087
  56.5 0.0 copy-done.1
  56.5 2.1 %collective-permute-start.1 = (f32[32,96]{1,0:T(8,128)S(1)}, f32[32,96]{1,0:T(8,128)S(1)}, u32[]{:S(2)}, u32[]{:S(2)}) collective-permute-start(f32[32,96]{1,0:T(8,128)S(1)} %copy-done.1), channel_id=1, source_target_pairs={{1,0},{2,1},{3,2},{0,3},{5,4},{6,5},{7,6},{4,7},{9,8},{10,9},{11,1... | collective-permute-start | bytes 36872 | tf_op jit(solution)/shard_map/ppermute | solution.py:1088
  58.5 18.5 %all-to-all-done.1.recv = f32[32,56,128]{2,1,0:T(8,128)S(1)} async-done(((f32[32,56,128]{2,1,0:T(8,128)}), f32[32,56,128]{2,1,0:T(8,128)S(1)}, u32[]{:S(2)}, u32[]{:S(2)}) %all-to-all-start.1) | async-done | bytes 917536 | tf_op jit(solution)/shard_map/all_to_all | solution.py:1063
  77.0 0.0 copy-done
  77.0 4.3 %finish_potential.1 = (f32[24,9216]{1,0:T(8,128)}, f32[32,128]{1,0:T(8,128)}) custom-call(f32[32,56,128]{2,1,0:T(8,128)S(1)} %all-to-all-done.1.recv, bf16[2048,192]{1,0:T(8,128)(2,1)S(1)} %copy-done, f32[8,24,9216]{2,1,0:T(8,128)} %history_h.1), custom_call_target="tpu_custom_call" | custom-call | flops 500000000 | bytes 10000000 | tf_op jit(solution)/shard_map/finish_potential/pallas_call | solution.py:1090
  81.4 4.8 %all-to-all-start.2 = ((f32[32,1,128]{2,1,0:T(1,128)}), f32[32,1,128]{2,1,0:T(1,128)S(1)}, u32[]{:S(2)}, u32[]{:S(2)}) async-start(f32[32,1,128]{2,1,0:T(1,128)} %bitcast.7), calls=%async_computation.2 | async-start | bytes 32768 | tf_op jit(solution)/shard_map/all_to_all | solution.py:1091
  86.2 0.0 collective-permute-done.below_h
  86.2 0.0 copy-start.4
  86.2 0.0 collective-permute-done.1.above_h
  86.2 0.0 copy-start.2
  86.2 0.6 copy-done.4
  86.8 0.0 copy-done.2
  86.8 5.5 %finish.1 = f32[24,9216]{1,0:T(8,128)} custom-call(f32[32,56,128]{2,1,0:T(8,128)} %all_to_all.19.recv, f32[24,9216]{1,0:T(8,128)} %get-tuple-element.10.partial_h, f32[16,96]{1,0:T(8,128)} %copy-done.4, f32[32,96]{1,0:T(8,128)} %copy-done.2, bf16[800,192]{1,0:T(8,128)(2,1)} %constant.10.clone.table_h), custom_call_target="tpu_custom_call" | custom-call | flops 3000000000 | bytes 4000000 | tf_op jit(solution)/shard_map/finish/pallas_call | solution.py:1089
  92.3 1.1 %all-to-all-done.2 = f32[32,1,128]{2,1,0:T(1,128)S(1)} async-done(((f32[32,1,128]{2,1,0:T(1,128)}), f32[32,1,128]{2,1,0:T(1,128)S(1)}, u32[]{:S(2)}, u32[]{:S(2)}) %all-to-all-start.2) | async-done | bytes 16416 | tf_op jit(solution)/shard_map/all_to_all | solution.py:1091
  93.3 0.6 reduce_sum.9
Async XLA Ops:
  50.1 4.6 %copy-start.3 = (f32[16,96]{1,0:T(8,128)S(1)}, f32[16,96]{1,0:T(8,128)}, u32[]{:S(2)}) copy-start(f32[16,96]{1,0:T(8,128)} %get-tuple-element.11) | copy-start | bytes 18436
  50.1 6.4 %copy-start.1 = (f32[32,96]{1,0:T(8,128)S(1)}, f32[32,96]{1,0:T(8,128)}, u32[]{:S(2)}) copy-start(f32[32,96]{1,0:T(8,128)} %get-tuple-element.12) | copy-start | bytes 36868
  50.1 26.9 %copy-start = (bf16[2048,192]{1,0:T(8,128)(2,1)S(1)}, bf16[2048,192]{1,0:T(8,128)(2,1)}, u32[]{:S(2)}) copy-start(bf16[2048,192]{1,0:T(8,128)(2,1)} %constant.12.clone.table_h) | copy-start | bytes 2359300
  50.1 26.9 %all-to-all-start.1 = ((f32[32,56,128]{2,1,0:T(8,128)}), f32[32,56,128]{2,1,0:T(8,128)S(1)}, u32[]{:S(2)}, u32[]{:S(2)}) async-start(f32[32,56,128]{2,1,0:T(8,128)} %bitcast.14), calls=%async_computation.1 | async-start | bytes 1835008 | tf_op jit(solution)/shard_map/all_to_all | solution.py:1063
  54.6 31.5 %collective-permute-start = (f32[16,96]{1,0:T(8,128)S(1)}, f32[16,96]{1,0:T(8,128)S(1)}, u32[]{:S(2)}, u32[]{:S(2)}) collective-permute-start(f32[16,96]{1,0:T(8,128)S(1)} %copy-done.3), channel_id=1, source_target_pairs={{0,1},{1,2},{2,3},{3,0},{4,5},{5,6},{6,7},{7,4},{8,9},{9,10},{10,1... | collective-permute-start | bytes 18440 | tf_op jit(solution)/shard_map/ppermute | solution.py:1087
  56.5 29.7 %collective-permute-start.1 = (f32[32,96]{1,0:T(8,128)S(1)}, f32[32,96]{1,0:T(8,128)S(1)}, u32[]{:S(2)}, u32[]{:S(2)}) collective-permute-start(f32[32,96]{1,0:T(8,128)S(1)} %copy-done.1), channel_id=1, source_target_pairs={{1,0},{2,1},{3,2},{0,3},{5,4},{6,5},{7,6},{4,7},{9,8},{10,9},{11,1... | collective-permute-start | bytes 36872 | tf_op jit(solution)/shard_map/ppermute | solution.py:1088
  81.4 12.0 %all-to-all-start.2 = ((f32[32,1,128]{2,1,0:T(1,128)}), f32[32,1,128]{2,1,0:T(1,128)S(1)}, u32[]{:S(2)}, u32[]{:S(2)}) async-start(f32[32,1,128]{2,1,0:T(1,128)} %bitcast.7), calls=%async_computation.2 | async-start | bytes 32768 | tf_op jit(solution)/shard_map/all_to_all | solution.py:1091
  86.2 0.6 copy-start.4
  86.2 0.6 copy-start.2

commit v3 on v2

--- a/solution.py
+++ b/solution.py
@@ -287,6 +287,7 @@
 PIECE = 40
 FACTS = 3 * PIECE
 VMEM_LIMIT = 60 * 1024 * 1024
+EARLY = 2
 LATE_LIMIT = 48 * 1024 * 1024
 
 
@@ -374,14 +375,11 @@
     x_window = np.zeros((count, length + GROUP, SUB), np.float32)
     x_of_row = (np.arange(length + GROUP) - SUB) % length
     padded = np.zeros((count, SUB, length))
-    kept = np.zeros((count, SUB, length))
-    donors = np.zeros((3, count, SUB, length))
     for d in range(count):
         for j in range(plan.j):
             mode = rows[j * count + d]
             x_window[d, :, j] = mode[x_of_row]
-            padded[d, j] = kept[d, j] = mode
-            donors[j // 2, d, 6 + j % 2] = mode
+            padded[d, j] = mode
         padded[d, 6:] = padded[d, 4:6]
     flat = lambda table: table.reshape(count * SUB, length)
     def halves_of(table):
@@ -425,7 +423,6 @@
             + halves_of(y_table)
             + halves_of(rows.T)
         ),
-        "c": pack(halves_of(np.stack([flat(kept)] + [flat(donors[i]) for i in range(3)]).reshape(-1, length))),
         "window": jnp.asarray(x_window.reshape(count, 1, -1)),
     }
 
@@ -776,8 +773,25 @@
                 0,
             )
 
-        backs = []
         energy = jnp.zeros((SUB, length), jnp.float32)
+        first = masks[0] == 0
+
+        def scatter(jp, b):
+            for yo in range(plan.yo):
+                at = b * plan.fy + yo * GROUP
+                found = []
+                for source in (main.at[2 * jp], main.at[2 * jp + 1], shared.at[jp]):
+                    upper, lower = block_turn(
+                        source[at : at + SUB, :], source[at + SUB : at + GROUP, :], masks
+                    )
+                    found.append(
+                        (jnp.where(first, upper, lower), jnp.where(first, lower, upper))
+                    )
+                for k in (0, 1):
+                    for zo, tile in enumerate((found[k][0], found[k][1], found[2][k])):
+                        ready[b, slot(yo * plan.zo + zo, jp, k)] = tile
+
+        rows_z = []
         for k in (0, 1):
             left = jnp.concatenate(
                 [
@@ -789,50 +803,28 @@
                 ],
                 0,
             )
-            rows_z = mm3(halves(left), (zt[0][k], zt[1][k]))
+            rows_z.append(mm3(halves(left), (zt[0][k], zt[1][k])))
+        for jp in range(plan.j // 2):
             rows_y = []
-            for jp in range(plan.j // 2):
+            for k in (0, 1):
                 j = 2 * jp + k
                 column = jnp.concatenate(
-                    [rows_z[jp * ext : (jp + 1) * ext], edges_z[j * GROUP : (j + 1) * GROUP]], 0
+                    [rows_z[k][jp * ext : (jp + 1) * ext], edges_z[j * GROUP : (j + 1) * GROUP]], 0
                 )
                 full = mm3((yt[0][0], yt[1][0]), halves(column))
-                squares = plane + square((2 * jp + k) * count + device)
+                squares = plane + square(j * count + device)
                 weight = jnp.where(squares > 0.0, scale / jnp.maximum(squares, 1.0), 0.0)
                 weighted = full * weight
                 product = full * weighted
                 for i in range(length // SUB):
                     energy += product[i * SUB : (i + 1) * SUB]
                 rows_y.append(mm3((yti[0][0], yti[1][0]), halves(weighted)))
-            backs.append(mm3(halves(jnp.concatenate(rows_y, 0)), (zt[0][k], zt[1][k]), NT))
-        for jp in range(plan.j // 2):
-            here = slice(jp * length, (jp + 1) * length)
+            backs = [mm3(halves(rows_y[k]), (zt[0][k], zt[1][k]), NT) for k in (0, 1)]
             for k in (0, 1):
-                main[2 * jp + k] = backs[k][here, :LANES]
-            shared[jp] = backs[0][here, LANES:] + backs[1][here, LANES:]
-
-        first = masks[0] == 0
-
-        def scatter(step, carry):
-            jp = step // plan.ny
-            b = lax.rem(step, plan.ny)
-            for yo in range(plan.yo):
-                at = pl.multiple_of(b * plan.fy + yo * GROUP, SUB)
-                found = []
-                for source in (main.at[2 * jp], main.at[2 * jp + 1], shared.at[jp]):
-                    upper, lower = block_turn(
-                        source[pl.ds(at, SUB), :], source[pl.ds(at + SUB, SUB), :], masks
-                    )
-                    found.append(
-                        (jnp.where(first, upper, lower), jnp.where(first, lower, upper))
-                    )
-                for k in (0, 1):
-                    for zo, tile in enumerate((found[k][0], found[k][1], found[2][k])):
-                        ready[b, slot(yo * plan.zo + zo, jp, k)] = tile
-            return carry
-
-        lax.fori_loop(0, plan.ny * (plan.j // 2), scatter, 0)
-
+                main[2 * jp + k] = backs[k][:, :LANES]
+            shared[jp] = backs[0][:, LANES:] + backs[1][:, LANES:]
+            for b in range(plan.ny):
+                scatter(jp, b)
         share = jnp.sum(energy) * (1.0 / count)
 
         def pack(b, carry):
@@ -984,18 +976,20 @@
     wide = 3 * LANES
 
     def kernel(
-        recv, table_h, history_h, potential_h, sums, tables_v, history, potential, sems
+        recv, early, table_h, history_h, potential_h, sums, tables_v, history, potential, sems
     ):
-        first = fetch([(table_h, tables_v)], sems)
-        copies = fetch([(history_h.at[i], history.at[i]) for i in range(terms)], sems, 2)
+        first = fetch([(table_h.at[: 2 * count * SUB, :], tables_v)], sems)
+        ahead = early.shape[0]
+        copies = [None] * ahead + fetch(
+            [(history_h.at[i], history.at[i - ahead]) for i in range(ahead, terms)], sems, 2
+        )
         first[0].wait()
         size = count * SUB
-        xb = [
-            [tables_v[(4 * h + i) * size : (4 * h + i + 1) * size, :] for i in range(4)]
-            for h in range(2)
-        ]
-        def modes(t):
-            return halves(recv[:, t * SUB : (t + 1) * SUB, :].reshape(count * SUB, LANES).T)
+        table = (tables_v[:size, :], tables_v[size:, :])
+        sub_row = lax.broadcasted_iota(jnp.int32, (count, SUB, LANES), 1)
+
+        def back(tile):
+            return mm3(halves(tile.reshape(size, LANES).T), table)
 
         def place(block, values):
             yo, zo = block // plan.zo, block % plan.zo
@@ -1006,23 +1000,26 @@
                     [rows[:SUB], rows[SUB:]], 1
                 )
 
-        given = [None, None]
+        spare = [jnp.zeros((count, SUB, LANES), jnp.float32)] * 2
         for t in range(per // SUB):
-            left = modes(t)
-            place(t, mm3(left, (xb[0][0], xb[1][0])))
+            tile = recv[:, t * SUB : (t + 1) * SUB, :]
+            place(t, back(jnp.where(sub_row < 6, tile, 0.0)))
             if t < 6:
-                part = mm3(left, (xb[0][1 + t % 3], xb[1][1 + t % 3]))
-                given[t // 3] = part if given[t // 3] is None else given[t // 3] + part
-        place(7, given[0])
-        place(8, given[1])
+                pair = t % 3
+                moved = pltpu.roll(tile, (2 * pair + 2) % SUB, 1)
+                spare[t // 3] = jnp.where(sub_row // 2 == pair, moved, spare[t // 3])
+        place(7, back(spare[0]))
+        place(8, back(spare[1]))
         out = fetch([(potential, potential_h)], sems, 2 + terms)
         acc = []
         for i in range(terms):
             def add(c, total, i=i):
                 cut = pl.ds(pl.multiple_of(c * wide, LANES), wide)
-                return total + history[i, :, cut] * potential[:, cut]
-
-            copies[i].wait()
+                other = early[i, :, cut] if i < ahead else history[i - ahead, :, cut]
+                return total + other * potential[:, cut]
+
+            if i >= ahead:
+                copies[i].wait()
             acc.append(
                 lax.fori_loop(
                     0, fy * length // wide, add, jnp.zeros((fz, wide), jnp.float32), unroll=4
@@ -1042,11 +1039,11 @@
     return pl.pallas_call(
         kernel,
         name="finish_potential",
-        in_specs=[vmem, hbm, hbm],
+        in_specs=[vmem, vmem, hbm, hbm],
         out_specs=[hbm, vmem],
         scratch_shapes=[
-            room(t["c"]),
-            pltpu.VMEM((terms, fz, fy * length), jnp.float32),
+            pltpu.VMEM((2 * count * SUB, length), jnp.bfloat16),
+            pltpu.VMEM((terms - EARLY, fz, fy * length), jnp.float32),
             pltpu.VMEM((fz, fy * length), jnp.float32),
             pltpu.SemaphoreType.DMA((3 + terms,)),
         ],
@@ -1082,12 +1079,14 @@
         spectra.reshape((plan.nz, plan.ny) + spectra.shape[1:]),
         tables_["b"],
     )
+    early, solved = lax.optimization_barrier((history, solved))
+    early = early[:EARLY]
     back = exchange(solved.reshape((count,) + solved.shape[2:]), axes)
     ring = [(i, (i + 1) % plan.ny) for i in range(plan.ny)]
     below = lax.ppermute(after, "gy", ring)
     above = lax.ppermute(before, "gy", [(target, source) for source, target in ring])
     residual = part_r(plan, tables_)(spectra, partial, below, above, tables_["a"])
-    potential, sums = part_c(plan, tables_, history.shape[0])(back, tables_["c"], history)
+    potential, sums = part_c(plan, tables_, history.shape[0])(back, early, tables_["a"], history)
     rows = lax.all_to_all(sums, axes, 0, 0, tiled=True)
     return residual, potential, jnp.sum(rows, 0)[: history.shape[0] + 1]
 

time: 94.3 us -> 91.2 us (0.967)
  Pallas kernels: 27.7 us -> 24.4 us
  local copies, waits for them, and re-layouts: 0.62 us -> 2.21 us
  waiting for transfers between devices: 19.5 us -> 18 us
    pallas_call x1, Pallas kernels: 12.8 us -> 10.1 us  [local_fast(): part_b(plan, tables_)]
    all_to_all x1, waiting for transfers between devices: 18.5 us -> 16.9 us  [exchange(): return lax.all_to_all(sent, axes, 0, 0, tiled=True)]
    slice x0 -> x1, local copies, waits for them, and re-layouts: none -> 1.59 us  [local_fast(): early = early[:EARLY]]
  transfers between devices with their start and end apart: 4 -> 4, of which waited for: 2 -> 2; matrix products, arithmetic and copies ran while one was open for 0% -> 2% of each run, Pallas kernels for 10% -> 10%
where the time goes in v3:
time: 91.2 us; the launch traced here: 90.6 us
  blocking collectives  29.7 us (33%)
  Pallas kernels  24.4 us (27%)
  waiting for transfers between devices  18 us (20%)
  starting transfers between devices  13.2 us (14%)
  between operations  2.68 us (3%)
  local copies, waits for them, and re-layouts  2.21 us (2%)
    all_to_all x1, blocking collectives, exchange(): return lax.all_to_all(sent, axes, 0, 0, tiled=True)  29.7 us
    all_to_all x1, waiting for transfers between devices, exchange(): return lax.all_to_all(sent, axes, 0, 0, tiled=True)  16.9 us
    pallas_call x1, Pallas kernels, local_fast(): part_b(plan, tables_)  10.1 us
    pallas_call x1, Pallas kernels, local_fast(): part_r(plan, tables_)(spectra, partial, below, above, tables_['a'])  5.49 us
    pallas_call x1, Pallas kernels, local_fast(): part_a(plan, tables_)  5.05 us
    all_to_all x1, starting transfers between devices, local_fast(): rows = lax.all_to_all(sums, axes, 0, 0, tiled=True)  4.78 us
    all_to_all x1, starting transfers between devices, exchange(): return lax.all_to_all(sent, axes, 0, 0, tiled=True)  4.51 us
    pallas_call x1, Pallas kernels, local_fast(): part_c(plan, tables_, history.shape[0])(back, early, tables_['a'], history)  3.77 us
  transfers between devices with their start and end apart: 4, of which 2 were waited for; matrix products, arithmetic and copies ran while one was open for 2% of the time, Pallas kernels for 10%

profile of v3, /device:TPU:0, one launch (start us, length us, event | category | flops | bytes accessed | tf_op | source)
XLA Modules:
  0.0 90.6 jit_solution(360037189825154287)
XLA Ops:
  2.6 5.0 %spread.1 = (f32[32,56,128]{2,1,0:T(8,128)}, f32[24,9216]{1,0:T(8,128)}, f32[16,96]{1,0:T(8,128)}, f32[32,96]{1,0:T(8,128)}) custom-call(s32[1]{0:T(128)} %bitcast.10.cell_h, f32[3]{0:T(128)} %bitcast.16, f32[1]{0:T(128)} %bitcast.11.charge_h, f32[1]{0:T(128)} %bitcast.12.width_h, f32[96,24,96]{2,1,0:T(8,128)} %coarse_h.1, f32[24,9216]{1,0:T(8,128)} %density_h.1, ...), custom_call_target="tpu_custom_call" | custom-call | flops 500000000 | bytes 4000000 | tf_op jit(solution)/shard_map/spread/pallas_call | solution.py:1067
  7.6 29.7 %all_to_all.19.recv = f32[32,56,128]{2,1,0:T(8,128)} all-to-all(f32[32,56,128]{2,1,0:T(8,128)} %get-tuple-element.11), channel_id=1, replica_groups=mesh['gz'=8,'gy'=4] {'gz','gy'}, dimensions={0} | all-to-all | bytes 1835008 | tf_op jit(solution)/shard_map/all_to_all | solution.py:1060
  37.3 10.1 %solve.1 = f32[8,4,56,128]{3,2,1,0:T(8,128)} custom-call(f32[32,1,1664]{2,1,0:T(1,128)} %constant.10.clone.window_h, f32[8,4,56,128]{3,2,1,0:T(8,128)} %bitcast.13, bf16[2560,240]{1,0:T(8,128)(2,1)} %constant.9.clone.table_h), custom_call_target="tpu_custom_call" | custom-call | flops 2000000000 | bytes 4000000 | tf_op jit(solution)/shard_map/solve/pallas_call | solution.py:1077
  47.4 0.0 copy-start.3
  47.4 0.0 copy-start.1
  47.4 4.5 %all-to-all-start.1 = ((f32[32,56,128]{2,1,0:T(8,128)}), f32[32,56,128]{2,1,0:T(8,128)S(1)}, u32[]{:S(2)}, u32[]{:S(2)}) async-start(f32[32,56,128]{2,1,0:T(8,128)} %bitcast.14), calls=%async_computation.1 | async-start | bytes 1835008 | tf_op jit(solution)/shard_map/all_to_all | solution.py:1060
  51.9 0.0 copy-done.3
  52.0 1.8 %collective-permute-start = (f32[16,96]{1,0:T(8,128)S(1)}, f32[16,96]{1,0:T(8,128)S(1)}, u32[]{:S(2)}, u32[]{:S(2)}) collective-permute-start(f32[16,96]{1,0:T(8,128)S(1)} %copy-done.3), channel_id=1, source_target_pairs={{0,1},{1,2},{2,3},{3,0},{4,5},{5,6},{6,7},{7,4},{8,9},{9,10},{10,1... | collective-permute-start | bytes 18440 | tf_op jit(solution)/shard_map/ppermute | solution.py:1086
  53.8 0.0 copy-done.1
  53.8 2.1 %collective-permute-start.1 = (f32[32,96]{1,0:T(8,128)S(1)}, f32[32,96]{1,0:T(8,128)S(1)}, u32[]{:S(2)}, u32[]{:S(2)}) collective-permute-start(f32[32,96]{1,0:T(8,128)S(1)} %copy-done.1), channel_id=1, source_target_pairs={{1,0},{2,1},{3,2},{0,3},{5,4},{6,5},{7,6},{4,7},{9,8},{10,9},{11,1... | collective-permute-start | bytes 36872 | tf_op jit(solution)/shard_map/ppermute | solution.py:1087
  55.8 1.6 %slice.6.early = f32[2,24,9216]{2,1,0:T(8,128)S(1)} slice(f32[8,24,9216]{2,1,0:T(8,128)} %history_h.1), slice={[0:2], [0:24], [0:9216]} | slice | bytes 3538944 | tf_op jit(solution)/shard_map/slice | solution.py:1083
  57.4 16.9 %all-to-all-done.1.recv = f32[32,56,128]{2,1,0:T(8,128)S(1)} async-done(((f32[32,56,128]{2,1,0:T(8,128)}), f32[32,56,128]{2,1,0:T(8,128)S(1)}, u32[]{:S(2)}, u32[]{:S(2)}) %all-to-all-start.1) | async-done | bytes 917536 | tf_op jit(solution)/shard_map/all_to_all | solution.py:1060
  74.3 0.0 copy-done
  74.3 3.8 %finish_potential.1 = (f32[24,9216]{1,0:T(8,128)}, f32[32,128]{1,0:T(8,128)}) custom-call(f32[32,56,128]{2,1,0:T(8,128)S(1)} %all-to-all-done.1.recv, f32[2,24,9216]{2,1,0:T(8,128)S(1)} %slice.6.early, bf16[800,192]{1,0:T(8,128)(2,1)S(1)} %copy-done, f32[8,24,9216]{2,1,0:T(8,128)} %history_h.1), custom_call_target="tpu_custom_call" | custom-call | flops 500000000 | bytes 10000000 | tf_op jit(solution)/shard_map/finish_potential/pallas_call | solution.py:1089
  78.1 4.8 %all-to-all-start.2 = ((f32[32,1,128]{2,1,0:T(1,128)}), f32[32,1,128]{2,1,0:T(1,128)S(1)}, u32[]{:S(2)}, u32[]{:S(2)}) async-start(f32[32,1,128]{2,1,0:T(1,128)} %bitcast.7), calls=%async_computation.2 | async-start | bytes 32768 | tf_op jit(solution)/shard_map/all_to_all | solution.py:1090
  82.9 0.0 collective-permute-done.below_h
  82.9 0.0 copy-start.4
  82.9 0.0 collective-permute-done.1.above_h
  82.9 0.0 copy-start.2
  82.9 0.6 copy-done.4
  83.5 0.0 copy-done.2
  83.5 5.5 %finish.1 = f32[24,9216]{1,0:T(8,128)} custom-call(f32[32,56,128]{2,1,0:T(8,128)} %all_to_all.19.recv, f32[24,9216]{1,0:T(8,128)} %get-tuple-element.12.partial_h, f32[16,96]{1,0:T(8,128)} %copy-done.4, f32[32,96]{1,0:T(8,128)} %copy-done.2, bf16[800,192]{1,0:T(8,128)(2,1)} %constant.8.clone.table_h), custom_call_target="tpu_custom_call" | custom-call | flops 3000000000 | bytes 4000000 | tf_op jit(solution)/shard_map/finish/pallas_call | solution.py:1088
  89.0 1.1 %all-to-all-done.2 = f32[32,1,128]{2,1,0:T(1,128)S(1)} async-done(((f32[32,1,128]{2,1,0:T(1,128)}), f32[32,1,128]{2,1,0:T(1,128)S(1)}, u32[]{:S(2)}, u32[]{:S(2)}) %all-to-all-start.2) | async-done | bytes 16416 | tf_op jit(solution)/shard_map/all_to_all | solution.py:1090
  90.1 0.6 reduce_sum.9
  (1 shorter events, 0.0 us)
Async XLA Ops:
  47.4 4.5 %copy-start.3 = (f32[16,96]{1,0:T(8,128)S(1)}, f32[16,96]{1,0:T(8,128)}, u32[]{:S(2)}) copy-start(f32[16,96]{1,0:T(8,128)} %get-tuple-element.13) | copy-start | bytes 18436
  47.4 6.4 %copy-start.1 = (f32[32,96]{1,0:T(8,128)S(1)}, f32[32,96]{1,0:T(8,128)}, u32[]{:S(2)}) copy-start(f32[32,96]{1,0:T(8,128)} %get-tuple-element.14) | copy-start | bytes 36868
  47.4 26.9 %all-to-all-start.1 = ((f32[32,56,128]{2,1,0:T(8,128)}), f32[32,56,128]{2,1,0:T(8,128)S(1)}, u32[]{:S(2)}, u32[]{:S(2)}) async-start(f32[32,56,128]{2,1,0:T(8,128)} %bitcast.14), calls=%async_computation.1 | async-start | bytes 1835008 | tf_op jit(solution)/shard_map/all_to_all | solution.py:1060
  52.0 30.9 %collective-permute-start = (f32[16,96]{1,0:T(8,128)S(1)}, f32[16,96]{1,0:T(8,128)S(1)}, u32[]{:S(2)}, u32[]{:S(2)}) collective-permute-start(f32[16,96]{1,0:T(8,128)S(1)} %copy-done.3), channel_id=1, source_target_pairs={{0,1},{1,2},{2,3},{3,0},{4,5},{5,6},{6,7},{7,4},{8,9},{9,10},{10,1... | collective-permute-start | bytes 18440 | tf_op jit(solution)/shard_map/ppermute | solution.py:1086
  53.8 20.5 %copy-start = (bf16[800,192]{1,0:T(8,128)(2,1)S(1)}, bf16[800,192]{1,0:T(8,128)(2,1)}, u32[]{:S(2)}) copy-start(bf16[800,192]{1,0:T(8,128)(2,1)} %constant.8.clone.table_h) | copy-start | bytes 921604
  53.8 29.1 %collective-permute-start.1 = (f32[32,96]{1,0:T(8,128)S(1)}, f32[32,96]{1,0:T(8,128)S(1)}, u32[]{:S(2)}, u32[]{:S(2)}) collective-permute-start(f32[32,96]{1,0:T(8,128)S(1)} %copy-done.1), channel_id=1, source_target_pairs={{1,0},{2,1},{3,2},{0,3},{5,4},{6,5},{7,6},{4,7},{9,8},{10,9},{11,1... | collective-permute-start | bytes 36872 | tf_op jit(solution)/shard_map/ppermute | solution.py:1087
  78.1 12.0 %all-to-all-start.2 = ((f32[32,1,128]{2,1,0:T(1,128)}), f32[32,1,128]{2,1,0:T(1,128)S(1)}, u32[]{:S(2)}, u32[]{:S(2)}) async-start(f32[32,1,128]{2,1,0:T(1,128)} %bitcast.7), calls=%async_computation.2 | async-start | bytes 32768 | tf_op jit(solution)/shard_map/all_to_all | solution.py:1090
  82.9 0.6 copy-start.4
  82.9 0.6 copy-start.2

commit v4 on v3

--- a/solution.py
+++ b/solution.py
@@ -288,6 +288,7 @@
 FACTS = 3 * PIECE
 VMEM_LIMIT = 60 * 1024 * 1024
 EARLY = 2
+SOLVE_LIMIT = 48 * 1024 * 1024
 LATE_LIMIT = 48 * 1024 * 1024
 
 
@@ -610,28 +611,22 @@
     per, per_back = plan.rows_out, plan.rows_back
 
     def kernel(
-        window_h, recv_h, table_h, send_h,
-        window, recv, tables_v, send, main, shared, bells, turned, ready, atoms_v, atoms, sem, sems, sems_in, sems_out,
+        window_h, recv, table_h, send_h,
+        window, tables_v, send, main, shared, bells, turned, ready, atoms_v, atoms, sem, sems, sems_out,
     ):
         device = lax.axis_index("gz") * plan.ny + lax.axis_index("gy")
 
-        def incoming(b):
-            return pltpu.make_async_copy(recv_h.at[:, b], recv.at[:, b], sems_in.at[b])
-
         def outgoing(b):
             return pltpu.make_async_copy(send.at[:, b], send_h.at[:, b], sems_out.at[b])
 
-        for b in range(plan.ny):
-            incoming(b).start()
         copies = fetch(
             [
-                (window_h.at[device], window),
+                (window_h.at[0], window),
                 (table_h, tables_v),
             ],
             sems,
         )
         def unpack(b, carry):
-            incoming(b).wait()
             for t in range(per // SUB):
                 tiles = turn_tiles(
                     [recv[a, b, t * SUB : (t + 1) * SUB, :] for a in range(plan.nz)]
@@ -828,8 +823,8 @@
         share = jnp.sum(energy) * (1.0 / count)
 
         def pack(b, carry):
-            for row in (SPARE, SPARE + 1):
-                ready[b, row] = jnp.full((SUB, LANES), share, jnp.float32)
+            ready[b, SPARE] = jnp.full((SUB, LANES), share, jnp.float32)
+            ready[b, SPARE + 1] = turned[b, SPARE]
             for t in range(per_back // SUB):
                 tiles = turn_tiles([ready[b, t * SUB + i] for i in range(SUB)])
                 for i, tile in enumerate(tiles):
@@ -847,13 +842,12 @@
     return pl.pallas_call(
         kernel,
         name="solve",
-        in_specs=[hbm, hbm, hbm],
+        in_specs=[hbm, pl.BlockSpec(memory_space=pltpu.VMEM), hbm],
         out_specs=hbm,
         out_shape=jax.ShapeDtypeStruct((plan.nz, plan.ny, per_back, LANES), jnp.float32),
-        compiler_params=pltpu.CompilerParams(vmem_limit_bytes=VMEM_LIMIT),
+        compiler_params=pltpu.CompilerParams(vmem_limit_bytes=SOLVE_LIMIT),
         scratch_shapes=[
             pltpu.SMEM(t["window"].shape[1:], jnp.float32),
-            pltpu.VMEM((plan.nz, plan.ny, per, LANES), jnp.float32),
             room(t["b"]),
             pltpu.VMEM((plan.nz, plan.ny, per_back, LANES), jnp.float32),
             pltpu.VMEM((plan.j, length, LANES), jnp.float32),
@@ -866,7 +860,6 @@
             pltpu.SemaphoreType.DMA,
             pltpu.SemaphoreType.DMA((2,)),
             pltpu.SemaphoreType.DMA((plan.ny,)),
-            pltpu.SemaphoreType.DMA((plan.ny,)),
         ],
         cost_estimate=pl.CostEstimate(flops=2_000_000_000, bytes_accessed=4_000_000, transcendentals=0),
     )
@@ -877,7 +870,7 @@
     per = plan.rows_out
 
     def kernel(
-        recv, partial_h, below_h, above_h, table_h, out_h,
+        solved, partial_h, below_h, above_h, table_h, out_h,
         partial, tables_v, out, field, lines, atoms_v, atoms, sem, sems,
     ):
         lines[...] = jnp.zeros_like(lines)
@@ -893,7 +886,7 @@
         a = lax.axis_index("gz")
         b = lax.axis_index("gy")
         for i in range(count):
-            atoms_v[i : i + 1, :] = recv[i, SPARE : SPARE + 1, :]
+            atoms_v[i : i + 1, :] = solved[i, SPARE + 1 : SPARE + 2, :]
         copy = pltpu.make_async_copy(atoms_v, atoms, sem)
         copy.start()
         for item in copies:
@@ -1074,18 +1067,21 @@
         tables_["a"],
     )
     spectra = exchange(sent, axes)
+    device = lax.axis_index("gz") * plan.ny + lax.axis_index("gy")
+    window = lax.dynamic_slice_in_dim(tables_["window"], device, 1, 0)
     solved = part_b(plan, tables_)(
-        tables_["window"],
+        window,
         spectra.reshape((plan.nz, plan.ny) + spectra.shape[1:]),
         tables_["b"],
     )
     early, solved = lax.optimization_barrier((history, solved))
     early = early[:EARLY]
-    back = exchange(solved.reshape((count,) + solved.shape[2:]), axes)
+    solved = solved.reshape((count,) + solved.shape[2:])
+    back = exchange(solved, axes)
     ring = [(i, (i + 1) % plan.ny) for i in range(plan.ny)]
     below = lax.ppermute(after, "gy", ring)
     above = lax.ppermute(before, "gy", [(target, source) for source, target in ring])
-    residual = part_r(plan, tables_)(spectra, partial, below, above, tables_["a"])
+    residual = part_r(plan, tables_)(solved, partial, below, above, tables_["a"])
     potential, sums = part_c(plan, tables_, history.shape[0])(back, early, tables_["a"], history)
     rows = lax.all_to_all(sums, axes, 0, 0, tiled=True)
     return residual, potential, jnp.sum(rows, 0)[: history.shape[0] + 1]

time: 91.2 us -> 90 us (0.987)
  blocking collectives: 29.7 us -> 0 us
  waiting for transfers between devices: 18 us -> 39.5 us
  starting transfers between devices: 13.2 us -> 20.5 us
  Pallas kernels: 24.4 us -> 23.4 us
    all_to_all x1 -> x0, blocking collectives: 29.7 us -> none  [exchange(): return lax.all_to_all(sent, axes, 0, 0, tiled=True)]
    all_to_all x1 -> x2, waiting for transfers between devices: 16.9 us -> 38.4 us  [exchange(): return lax.all_to_all(sent, axes, 0, 0, tiled=True)]
    all_to_all x1 -> x2, starting transfers between devices: 4.51 us -> 11.9 us  [exchange(): return lax.all_to_all(sent, axes, 0, 0, tiled=True)]
    pallas_call x1, Pallas kernels: 10.1 us -> 8.99 us  [local_fast(): part_b(plan, tables_)]
  transfers between devices with their start and end apart: 4 -> 5, of which waited for: 2 -> 3; matrix products, arithmetic and copies ran while one was open for 2% -> 3% of each run, Pallas kernels for 10% -> 10%
where the time goes in v4:
time: 90 us; the launch traced here: 89.5 us
  waiting for transfers between devices  39.5 us (44%)
  Pallas kernels  23.4 us (26%)
  starting transfers between devices  20.5 us (23%)
  local copies, waits for them, and re-layouts  2.91 us (3%)
  between operations  2.7 us (3%)
    all_to_all x2, waiting for transfers between devices, exchange(): return lax.all_to_all(sent, axes, 0, 0, tiled=True)  38.4 us
    all_to_all x2, starting transfers between devices, exchange(): return lax.all_to_all(sent, axes, 0, 0, tiled=True)  11.9 us
    pallas_call x1, Pallas kernels, local_fast(): part_b(plan, tables_)  8.99 us
    pallas_call x1, Pallas kernels, local_fast(): part_r(plan, tables_)(solved, partial, below, above, tables_['a'])  5.49 us
    pallas_call x1, Pallas kernels, local_fast(): part_a(plan, tables_)  5.12 us
    all_to_all x1, starting transfers between devices, local_fast(): rows = lax.all_to_all(sums, axes, 0, 0, tiled=True)  4.78 us
    pallas_call x1, Pallas kernels, local_fast(): part_c(plan, tables_, history.shape[0])(back, early, tables_['a'], history)  3.77 us
    ppermute x1, starting transfers between devices, local_fast(): lax.ppermute(before, 'gy', [(target, source) for source, target in ring])  2.05 us
  transfers between devices with their start and end apart: 5, of which 3 were waited for; matrix products, arithmetic and copies ran while one was open for 3% of the time, Pallas kernels for 10%

profile of v4, /device:TPU:0, one launch (start us, length us, event | category | flops | bytes accessed | tf_op | source)
XLA Modules:
  0.0 89.5 jit_solution(14126567108473123143)
XLA Ops:
  2.6 0.0 copy-start.1
  2.6 5.1 %spread.1 = (f32[32,56,128]{2,1,0:T(8,128)}, f32[24,9216]{1,0:T(8,128)}, f32[16,96]{1,0:T(8,128)}, f32[32,96]{1,0:T(8,128)}) custom-call(s32[1]{0:T(128)} %bitcast.10.cell_h, f32[3]{0:T(128)} %bitcast.15, f32[1]{0:T(128)} %bitcast.11.charge_h, f32[1]{0:T(128)} %bitcast.12.width_h, f32[96,24,96]{2,1,0:T(8,128)} %coarse_h.1, f32[24,9216]{1,0:T(8,128)} %density_h.1, ...), custom_call_target="tpu_custom_call" | custom-call | flops 500000000 | bytes 4000000 | tf_op jit(solution)/shard_map/spread/pallas_call | solution.py:1060
  7.7 7.3 %all-to-all-start = ((f32[32,56,128]{2,1,0:T(8,128)}), f32[32,56,128]{2,1,0:T(8,128)S(1)}, u32[]{:S(2)}, u32[]{:S(2)}) async-start(f32[32,56,128]{2,1,0:T(8,128)} %get-tuple-element.11), calls=%async_computation | async-start | bytes 1835008 | tf_op jit(solution)/shard_map/all_to_all | solution.py:1053
  15.1 0.7 constant_dynamic-slice_fusion.window_h
  15.8 21.5 %all-to-all-done = f32[32,56,128]{2,1,0:T(8,128)S(1)} async-done(((f32[32,56,128]{2,1,0:T(8,128)}), f32[32,56,128]{2,1,0:T(8,128)S(1)}, u32[]{:S(2)}, u32[]{:S(2)}) %all-to-all-start) | async-done | bytes 917536 | tf_op jit(solution)/shard_map/all_to_all | solution.py:1053
  37.3 0.0 copy-done.1
  37.3 9.0 %solve.1 = f32[8,4,56,128]{3,2,1,0:T(8,128)} custom-call(f32[1,1,1664]{2,1,0:T(1,128)S(1)} %constant_dynamic-slice_fusion.window_h, f32[8,4,56,128]{3,2,1,0:T(8,128)S(1)} %bitcast.13, bf16[2560,240]{1,0:T(8,128)(2,1)S(1)} %copy-done.1), custom_call_target="tpu_custom_call" | custom-call | flops 2000000000 | bytes 4000000 | tf_op jit(solution)/shard_map/solve/pallas_call | solution.py:1072
  46.3 0.0 copy-start.4
  46.3 0.0 copy-start.2
  46.3 4.5 %all-to-all-start.1 = ((f32[32,56,128]{2,1,0:T(8,128)}), f32[32,56,128]{2,1,0:T(8,128)S(1)}, u32[]{:S(2)}, u32[]{:S(2)}) async-start(f32[32,56,128]{2,1,0:T(8,128)} %bitcast.5.solved), calls=%async_computation.1 | async-start | bytes 1835008 | tf_op jit(solution)/shard_map/all_to_all | solution.py:1053
  50.8 1.8 %collective-permute-start = (f32[16,96]{1,0:T(8,128)S(1)}, f32[16,96]{1,0:T(8,128)S(1)}, u32[]{:S(2)}, u32[]{:S(2)}) collective-permute-start(f32[16,96]{1,0:T(8,128)S(1)} %copy-done.4), channel_id=1, source_target_pairs={{0,1},{1,2},{2,3},{3,0},{4,5},{5,6},{6,7},{7,4},{8,9},{9,10},{10,1... | collective-permute-start | bytes 18440 | tf_op jit(solution)/shard_map/ppermute | solution.py:1082
  52.6 2.1 %collective-permute-start.1 = (f32[32,96]{1,0:T(8,128)S(1)}, f32[32,96]{1,0:T(8,128)S(1)}, u32[]{:S(2)}, u32[]{:S(2)}) collective-permute-start(f32[32,96]{1,0:T(8,128)S(1)} %copy-done.2), channel_id=1, source_target_pairs={{1,0},{2,1},{3,2},{0,3},{5,4},{6,5},{7,6},{4,7},{9,8},{10,9},{11,1... | collective-permute-start | bytes 36872 | tf_op jit(solution)/shard_map/ppermute | solution.py:1083
  54.7 1.6 %slice.6.early = f32[2,24,9216]{2,1,0:T(8,128)S(1)} slice(f32[8,24,9216]{2,1,0:T(8,128)} %history_h.1), slice={[0:2], [0:24], [0:9216]} | slice | bytes 3538944 | tf_op jit(solution)/shard_map/slice | solution.py:1078
  56.3 16.9 %all-to-all-done.1.recv = f32[32,56,128]{2,1,0:T(8,128)S(1)} async-done(((f32[32,56,128]{2,1,0:T(8,128)}), f32[32,56,128]{2,1,0:T(8,128)S(1)}, u32[]{:S(2)}, u32[]{:S(2)}) %all-to-all-start.1) | async-done | bytes 917536 | tf_op jit(solution)/shard_map/all_to_all | solution.py:1053
  73.2 3.8 %finish_potential.1 = (f32[24,9216]{1,0:T(8,128)}, f32[32,128]{1,0:T(8,128)}) custom-call(f32[32,56,128]{2,1,0:T(8,128)S(1)} %all-to-all-done.1.recv, f32[2,24,9216]{2,1,0:T(8,128)S(1)} %slice.6.early, bf16[800,192]{1,0:T(8,128)(2,1)S(1)} %copy-done, f32[8,24,9216]{2,1,0:T(8,128)} %history_h.1), custom_call_target="tpu_custom_call" | custom-call | flops 500000000 | bytes 10000000 | tf_op jit(solution)/shard_map/finish_potential/pallas_call | solution.py:1085
  77.0 4.8 %all-to-all-start.2 = ((f32[32,1,128]{2,1,0:T(1,128)}), f32[32,1,128]{2,1,0:T(1,128)S(1)}, u32[]{:S(2)}, u32[]{:S(2)}) async-start(f32[32,1,128]{2,1,0:T(1,128)} %bitcast.7), calls=%async_computation.2 | async-start | bytes 32768 | tf_op jit(solution)/shard_map/all_to_all | solution.py:1086
  81.8 0.0 collective-permute-done.below_h
  81.8 0.0 collective-permute-done.1.above_h
  81.8 0.0 copy-start.3
  81.8 0.6 copy-done.5
  82.4 0.0 copy-done.3
  82.4 5.5 %finish.1 = f32[24,9216]{1,0:T(8,128)} custom-call(f32[32,56,128]{2,1,0:T(8,128)} %bitcast.5.solved, f32[24,9216]{1,0:T(8,128)} %get-tuple-element.13.partial_h, f32[16,96]{1,0:T(8,128)} %copy-done.5, f32[32,96]{1,0:T(8,128)} %copy-done.3, bf16[800,192]{1,0:T(8,128)(2,1)} %constant.23.clone.table_h), custom_call_target="tpu_custom_call" | custom-call | flops 3000000000 | bytes 4000000 | tf_op jit(solution)/shard_map/finish/pallas_call | solution.py:1084
  87.9 1.1 %all-to-all-done.2 = f32[32,1,128]{2,1,0:T(1,128)S(1)} async-done(((f32[32,1,128]{2,1,0:T(1,128)}), f32[32,1,128]{2,1,0:T(1,128)S(1)}, u32[]{:S(2)}, u32[]{:S(2)}) %all-to-all-start.2) | async-done | bytes 16416 | tf_op jit(solution)/shard_map/all_to_all | solution.py:1086
  88.9 0.6 reduce_sum.9
  (5 shorter events, 0.0 us)
Async XLA Ops:
  2.6 34.7 %copy-start.1 = (bf16[2560,240]{1,0:T(8,128)(2,1)S(1)}, bf16[2560,240]{1,0:T(8,128)(2,1)}, u32[]{:S(2)}) copy-start(bf16[2560,240]{1,0:T(8,128)(2,1)} %constant.24.clone.table_h) | copy-start | bytes 3686404
  7.7 29.6 %all-to-all-start = ((f32[32,56,128]{2,1,0:T(8,128)}), f32[32,56,128]{2,1,0:T(8,128)S(1)}, u32[]{:S(2)}, u32[]{:S(2)}) async-start(f32[32,56,128]{2,1,0:T(8,128)} %get-tuple-element.11), calls=%async_computation | async-start | bytes 1835008 | tf_op jit(solution)/shard_map/all_to_all | solution.py:1053
  46.3 4.6 %copy-start.4 = (f32[16,96]{1,0:T(8,128)S(1)}, f32[16,96]{1,0:T(8,128)}, u32[]{:S(2)}) copy-start(f32[16,96]{1,0:T(8,128)} %get-tuple-element.14) | copy-start | bytes 18436
  46.3 6.4 %copy-start.2 = (f32[32,96]{1,0:T(8,128)S(1)}, f32[32,96]{1,0:T(8,128)}, u32[]{:S(2)}) copy-start(f32[32,96]{1,0:T(8,128)} %get-tuple-element.15) | copy-start | bytes 36868
  46.3 26.9 %all-to-all-start.1 = ((f32[32,56,128]{2,1,0:T(8,128)}), f32[32,56,128]{2,1,0:T(8,128)S(1)}, u32[]{:S(2)}, u32[]{:S(2)}) async-start(f32[32,56,128]{2,1,0:T(8,128)} %bitcast.5.solved), calls=%async_computation.1 | async-start | bytes 1835008 | tf_op jit(solution)/shard_map/all_to_all | solution.py:1053
  50.8 30.9 %collective-permute-start = (f32[16,96]{1,0:T(8,128)S(1)}, f32[16,96]{1,0:T(8,128)S(1)}, u32[]{:S(2)}, u32[]{:S(2)}) collective-permute-start(f32[16,96]{1,0:T(8,128)S(1)} %copy-done.4), channel_id=1, source_target_pairs={{0,1},{1,2},{2,3},{3,0},{4,5},{5,6},{6,7},{7,4},{8,9},{9,10},{10,1... | collective-permute-start | bytes 18440 | tf_op jit(solution)/shard_map/ppermute | solution.py:1082
  52.6 20.5 %copy-start = (bf16[800,192]{1,0:T(8,128)(2,1)S(1)}, bf16[800,192]{1,0:T(8,128)(2,1)}, u32[]{:S(2)}) copy-start(bf16[800,192]{1,0:T(8,128)(2,1)} %constant.23.clone.table_h) | copy-start | bytes 921604
  52.6 29.1 %collective-permute-start.1 = (f32[32,96]{1,0:T(8,128)S(1)}, f32[32,96]{1,0:T(8,128)S(1)}, u32[]{:S(2)}, u32[]{:S(2)}) collective-permute-start(f32[32,96]{1,0:T(8,128)S(1)} %copy-done.2), channel_id=1, source_target_pairs={{1,0},{2,1},{3,2},{0,3},{5,4},{6,5},{7,6},{4,7},{9,8},{10,9},{11,1... | collective-permute-start | bytes 36872 | tf_op jit(solution)/shard_map/ppermute | solution.py:1083
  77.0 12.0 %all-to-all-start.2 = ((f32[32,1,128]{2,1,0:T(1,128)}), f32[32,1,128]{2,1,0:T(1,128)S(1)}, u32[]{:S(2)}, u32[]{:S(2)}) async-start(f32[32,1,128]{2,1,0:T(1,128)} %bitcast.7), calls=%async_computation.2 | async-start | bytes 32768 | tf_op jit(solution)/shard_map/all_to_all | solution.py:1086
  81.8 0.6 copy-start.5
  81.8 0.6 copy-start.3
